TPU v7x, 256 devices: a whole 4x4x8 slice. The times are simulated.
256 devices in a mesh: mem: 8 (over z_lo, y), col: 32 (over z_hi, x, core).
Axes of the slice: x: 4, y: 4, z: 8 (z_hi: 4, z_lo: 2; z = z_hi * 2 + z_lo), core: 2. Of those that a mesh axis runs over, the one named last changes fastest.
Arguments:
- perturbations: bfloat16 [4, 256, 512, 256], P(None, 'mem', 'col'), may hold values from -4 to 4
- loc_weights: float32 [7], replicated, may hold values from 0.3 to 1
- offsets: int32 [7, 2], replicated, may hold values from -4 to 4, as said below
- obs_x: int32 [65536], P('col'), may hold values from 0 to 511, as said below
- obs_y: int32 [65536], P('col'), may hold values from 0 to 255
- obs_t: int32 [65536], P('col'), may hold values from 0 to 3
- innovations: float32 [65536], P('col'), may hold values from -6 to 6
- obs_rinv: float32 [65536], P('col'), may hold values from 0.5 to 6
Outputs:
- control: float32 [256, 512, 256], P('mem', 'col')
- increment: float32 [4, 512, 256], P(None, 'col')
Inputs may be any that keep to these rules, and one draw needn't show every extreme that they name: `obs_x`: observation o lies in the columns (o // 2048) * 16 to (o // 2048) * 16 + 15. `offsets`: column 0 gives the offset along the first grid dimension, column 1 along the second; along the first both -4 and 4 occur.
All inputs are finite; a program needn't handle non-finite values.
Results may differ from a plain program's by a relative error of at most 0.00035.
Values may be sent and summed in bfloat16 or wider, within the bound.
A program may use at most 64 MiB of HBM per device.

v0:
```python
import jax
import jax.numpy as jnp
from jax import lax
from jax.experimental import pallas as pl
from jax.experimental.pallas import tpu as pltpu
from jax.sharding import PartitionSpec as P

TAPS = 7
RADIUS = 4
LANES = 128
HALO = 2 * RADIUS
F32 = jnp.float32
MESH = pl.DeviceIdType.MESH


def make_kernel(groups, blocks, levels, members, width, depth, obs_rows):
    halves = depth // LANES
    planes = levels * halves
    rows = width + 2 * HALO
    own = pl.ds(HALO, width)
    low_rows = pl.ds(0, HALO)
    high_rows = pl.ds(HALO + width, HALO)
    last_own = pl.ds(width, HALO)
    first_own = pl.ds(HALO, HALO)

    def kernel(
        pert, weights, offsets, obs_x, obs_y, obs_t, innov, rinv,
        control, increment,
        p, p_low, p_high, fields, z, mixed, resid, second, part, gathered, full,
        note, group_note, sums, block_note,
        load_sem, halo_send, halo_recv, field_send, field_recv,
        rs_send, rs_recv, ag_send, ag_recv, low_send, low_recv, high_send, high_recv,
        note_send, note_recv, sum_send, sum_recv,
    ):
        me = lax.axis_index("mem")
        col = lax.axis_index("col")
        right = lax.rem(col + 1, blocks)
        left = lax.rem(col + blocks - 1, blocks)

        barrier = pltpu.get_barrier_semaphore()

        def greet(target):
            pl.semaphore_signal(barrier, inc=1, device_id=target, device_id_type=MESH)

        load = pltpu.make_async_copy(pert, p, load_sem)
        load.start()
        for step in range(1, groups):
            greet((lax.rem(me + step, groups), col))
        for other in range(groups):
            greet((other, right))
            greet((other, left))

        def greet_block(step, carry):
            greet((me, lax.rem(col + step, blocks)))
            return carry

        lax.fori_loop(1, blocks, greet_block, 0)

        lanes8 = lax.broadcasted_iota(jnp.int32, (1, LANES), 1)
        cell_rows = lax.broadcasted_iota(jnp.int32, (levels * width, LANES), 0)
        depth_rows = lax.broadcasted_iota(jnp.int32, (depth, LANES), 0)

        def place(chunk, total):
            at = pl.ds(chunk, 1)
            cell = obs_t[at, :] * width + (obs_x[at, :] - col * width)
            r = rinv[at, :]
            hit = cell_rows == cell
            pieces = []
            for value in (r * innov[at, :], r):
                rest = value
                for _ in range(3):
                    piece = rest.astype(jnp.bfloat16)
                    rest = rest - piece.astype(F32)
                    pieces.append(jnp.where(hit, piece.astype(F32), 0.0).astype(jnp.bfloat16))
            left_side = jnp.concatenate(pieces, axis=0)
            right_side = jnp.where(depth_rows == obs_y[at, :], 1.0, 0.0).astype(jnp.bfloat16)
            return total + lax.dot_general(
                left_side, right_side, (((1,), (1,)), ((), ())), preferred_element_type=F32
            )

        spread = lax.fori_loop(
            0, obs_rows, place, jnp.zeros((6 * levels * width, depth), F32)
        )
        cells = levels * width
        for which in range(2):
            base = 3 * which * cells
            summed = (
                spread[base : base + cells]
                + spread[base + cells : base + 2 * cells]
                + spread[base + 2 * cells : base + 3 * cells]
            )
            for level in range(levels):
                for half in range(halves):
                    fields[which, level * halves + half, own, :] = summed[
                        level * width : (level + 1) * width, half * LANES : (half + 1) * LANES
                    ]

        pl.semaphore_wait(barrier, groups - 1 + 2 * groups + blocks - 1)

        def remote(source, target, send, recv, device):
            return pltpu.make_async_remote_copy(
                src_ref=source, dst_ref=target, send_sem=send, recv_sem=recv,
                device_id=device, device_id_type=MESH,
            )

        to_right = remote(
            pert.at[:, :, pl.ds(width - HALO, HALO), :], p_low, halo_send.at[0], halo_recv.at[0], (me, right)
        )
        to_left = remote(
            pert.at[:, :, pl.ds(0, HALO), :], p_high, halo_send.at[1], halo_recv.at[1], (me, left)
        )
        to_right.start()
        to_left.start()
        fields_right = remote(
            fields.at[:, :, last_own, :], fields.at[:, :, low_rows, :],
            field_send.at[0], field_recv.at[0], (me, right),
        )
        fields_left = remote(
            fields.at[:, :, first_own, :], fields.at[:, :, high_rows, :],
            field_send.at[1], field_recv.at[1], (me, left),
        )
        fields_right.start()
        fields_left.start()

        tap_weight = [weights[s] for s in range(TAPS)]
        along = [offsets[2 * s] for s in range(TAPS)]
        across = [offsets[2 * s + 1] for s in range(TAPS)]

        def shifted(pair, amount):
            turn = jnp.where(amount < 0, amount + LANES, amount)
            turned = [pltpu.roll(v, turn, 1) for v in pair]
            spot = lax.broadcasted_iota(jnp.int32, pair[0].shape, 1) - amount
            inside = (spot >= 0) & (spot < LANES)
            return [
                jnp.where(inside, turned[h], turned[1 - h]) for h in range(halves)
            ]

        def mix(source, at, k):
            for half in range(halves):
                total = None
                for level in range(levels):
                    term = source[level, k, :, half * LANES : (half + 1) * LANES].astype(F32) * z[
                        level * halves + half, at, :
                    ]
                    total = term if total is None else total + term
                mixed[k, half, at, :] = total

        def mix_own():
            def step(k, carry):
                for more in range(2):
                    mix(p, own, 2 * k + more)
                return carry

            lax.fori_loop(0, members // 2, step, 0)

        def mix_edges():
            def step(k, carry):
                for more in range(2):
                    mix(p_low, low_rows, 2 * k + more)
                    mix(p_high, high_rows, 2 * k + more)
                return carry

            lax.fori_loop(0, members // 2, step, 0)

        reach = width + 2 * RADIUS
        row_at = lax.broadcasted_iota(jnp.int32, (reach, LANES), 0) + (col * width - RADIUS)
        keep = jnp.where((row_at >= 0) & (row_at < blocks * width), 1.0, 0.0)

        def transpose_taps(turn):
            def step(k, carry):
                total = [jnp.zeros((reach, LANES), F32) for _ in range(halves)]
                for s in range(TAPS):
                    start = RADIUS - along[s]
                    pair = [mixed[k, half, pl.ds(start, reach), :] for half in range(halves)]
                    moved = shifted(pair, across[s])
                    total = [total[half] + tap_weight[s] * moved[half] for half in range(halves)]
                for half in range(halves):
                    resid[turn, k, half, pl.ds(RADIUS, reach), :] = total[half] * keep
                return carry

            lax.fori_loop(0, members, step, 0)

        def taps_and_sum(turn):
            def step(k, sums_so_far):
                total = [jnp.zeros((width, LANES), F32) for _ in range(halves)]
                for s in range(TAPS):
                    start = HALO + along[s]
                    pair = [resid[turn, k, half, pl.ds(start, width), :] for half in range(halves)]
                    moved = shifted(pair, -across[s])
                    total = [total[half] + tap_weight[s] * moved[half] for half in range(halves)]
                return tuple(
                    sums_so_far[level * halves + half]
                    + p[level, k, :, half * LANES : (half + 1) * LANES].astype(F32) * total[half]
                    for level in range(levels)
                    for half in range(halves)
                )

            summed = lax.fori_loop(
                0, members, step, tuple(jnp.zeros((width, LANES), F32) for _ in range(planes))
            )
            for plane in range(planes):
                part[turn, plane] = summed[plane]

        def chunk_copy(turn, step):
            peer = lax.rem(me + step, groups)
            return remote(
                part.at[turn, peer], gathered.at[turn, step - 1],
                rs_send.at[turn, step - 1], rs_recv.at[turn, step - 1], (peer, col),
            )

        def whole_copy(turn, step, sender, peer):
            spot = full.at[turn, sender, own, :]
            return remote(
                spot, spot, ag_send.at[turn, step - 1], ag_recv.at[turn, step - 1], (peer, col)
            )

        def edge_copies(turn, other, sender, slot):
            return (
                remote(
                    full.at[turn, sender, last_own, :], full.at[turn, sender, low_rows, :],
                    low_send.at[turn, other], low_recv.at[turn, slot], (other, right),
                ),
                remote(
                    full.at[turn, sender, first_own, :], full.at[turn, sender, high_rows, :],
                    high_send.at[turn, other], high_recv.at[turn, slot], (other, left),
                ),
            )

        def note_copy(which, step, sender, peer):
            return remote(
                note.at[which], group_note.at[which, sender],
                note_send.at[which, step - 1], note_recv.at[which, step - 1], (peer, col),
            )

        def sum_copy(which, step, sender, peer):
            return remote(
                sums.at[which], block_note.at[which, sender],
                sum_send.at[which, step - 1], sum_recv.at[which, step - 1], (me, peer),
            )

        def start_sums(turn):
            def step(s, carry):
                chunk_copy(turn, s).start()
                return carry

            lax.fori_loop(1, groups, step, 0)

        def finish_sums(turn):
            def step(s, carry):
                chunk_copy(turn, s).wait_recv()
                return carry

            lax.fori_loop(1, groups, step, 0)
            total = part[turn, me]
            for s in range(groups - 1):
                total = total + gathered[turn, s]
            full[turn, me, own, :] = total
            return total

        def start_spread(turn, edges):
            def step(s, carry):
                whole_copy(turn, s, me, lax.rem(me + s, groups)).start()
                return carry

            lax.fori_loop(1, groups, step, 0)
            if edges:

                def edge_step(other, carry):
                    for copy in edge_copies(turn, other, me, me):
                        copy.start()
                    return carry

                lax.fori_loop(0, groups, edge_step, 0)

        def finish_own(turn):
            def step(s, carry):
                peer = lax.rem(me + groups - s, groups)
                whole_copy(turn, s, peer, peer).wait_recv()
                return carry

            lax.fori_loop(1, groups, step, 0)

        def finish_edges(turn):
            def step(other, carry):
                for copy in edge_copies(turn, other, other, other):
                    copy.wait_recv()
                return carry

            lax.fori_loop(0, groups, step, 0)

        def send_note(which, values):
            row = jnp.zeros((1, LANES), F32)
            for at, value in enumerate(values):
                row = jnp.where(lanes8 == at, value, row)
            note[which] = row
            group_note[which, me] = row

            def step(s, carry):
                note_copy(which, s, me, lax.rem(me + s, groups)).start()
                return carry

            lax.fori_loop(1, groups, step, 0)

        def pass_note(which):
            def step(s, carry):
                peer = lax.rem(me + groups - s, groups)
                note_copy(which, s, peer, peer).wait_recv()
                return carry

            lax.fori_loop(1, groups, step, 0)
            total = group_note[which, 0]
            for other in range(1, groups):
                total = total + group_note[which, other]
            sums[which] = total
            block_note[which, col] = total

            def send(s, carry):
                sum_copy(which, s, col, lax.rem(col + s, blocks)).start()
                return carry

            lax.fori_loop(1, blocks, send, 0)

        def read_note(which, count):
            def step(s, carry):
                peer = lax.rem(col + blocks - s, blocks)
                sum_copy(which, s, peer, peer).wait_recv()
                return carry

            lax.fori_loop(1, blocks, step, 0)
            total = block_note[which, 0]
            for other in range(1, blocks):
                total = total + block_note[which, other]
            return [
                jnp.sum(jnp.where(lanes8 == at, total, 0.0), axis=1, keepdims=True)
                for at in range(count)
            ]

        def all_of(value):
            return jnp.sum(jnp.sum(value, axis=0, keepdims=True), axis=1, keepdims=True)

        load.wait()
        for plane in range(planes):
            z[plane, own, :] = fields[0, plane, own, :]
        mix_own()
        fields_right.wait_recv()
        fields_left.wait_recv()
        has_left = jnp.where(col > 0, 1.0, 0.0)
        has_right = jnp.where(col < blocks - 1, 1.0, 0.0)
        for which in range(2):
            for plane in range(planes):
                fields[which, plane, low_rows, :] = fields[which, plane, low_rows, :] * has_left
                fields[which, plane, high_rows, :] = fields[which, plane, high_rows, :] * has_right
        for plane in range(planes):
            z[plane, low_rows, :] = fields[0, plane, low_rows, :]
            z[plane, high_rows, :] = fields[0, plane, high_rows, :]
        to_right.wait_recv()
        to_left.wait_recv()
        mix_edges()
        transpose_taps(0)
        taps_and_sum(0)
        start_sums(0)

        def square(k, total):
            for half in range(halves):
                value = resid[0, k, half, own, :]
                total = total + value * value
            return total

        norm = all_of(lax.fori_loop(0, members, square, jnp.zeros((width, LANES), F32)))
        mine = finish_sums(0)
        start_spread(0, True)
        send_note(0, [norm, all_of(fields[1, me, own, :] * mine * mine)])
        finish_own(0)
        pass_note(0)

        def image_of_first(at):
            for plane in range(planes):
                z[plane, at, :] = (
                    fields[0, plane, at, :] + fields[1, plane, at, :] * full[0, plane, at, :]
                )

        image_of_first(own)
        mix_own()
        finish_edges(0)
        image_of_first(low_rows)
        image_of_first(high_rows)
        mix_edges()
        transpose_taps(1)
        taps_and_sum(1)
        start_sums(1)
        finish_sums(1)
        start_spread(1, True)
        norm_0, bend_0 = read_note(0, 2)
        curve_0 = norm_0 + bend_0
        step_0 = norm_0 / curve_0
        finish_own(1)

        def image_of_second(at):
            for plane in range(planes):
                z[plane, at, :] = (fields[0, plane, at, :] - step_0 * z[plane, at, :]) + fields[
                    1, plane, at, :
                ] * (full[0, plane, at, :] - step_0 * full[1, plane, at, :])

        image_of_second(own)
        mix_own()
        finish_edges(1)
        image_of_second(low_rows)
        image_of_second(high_rows)
        mix_edges()
        transpose_taps(2)
        taps_and_sum(2)
        start_sums(2)

        def products(k, so_far):
            ab, ac, bb, bc, cc = so_far
            for half in range(halves):
                a = resid[0, k, half, own, :]
                b = a - step_0 * resid[1, k, half, own, :]
                c = resid[2, k, half, own, :]
                second[k, half] = b
                ab, ac, bb, bc, cc = ab + a * b, ac + a * c, bb + b * b, bc + b * c, cc + c * c
            return ab, ac, bb, bc, cc

        inner = [
            all_of(v)
            for v in lax.fori_loop(
                0, members, products, tuple(jnp.zeros((width, LANES), F32) for _ in range(5))
            )
        ]
        mine_c = finish_sums(2)
        start_spread(2, False)
        mine_a = full[0, me, own, :]
        mine_b = mine_a - step_0 * full[1, me, own, :]
        weight = fields[1, me, own, :]
        wb, wc = weight * mine_b, weight * mine_c
        bends = [all_of(v) for v in (wb * mine_a, wc * mine_a, wb * mine_b, wc * mine_b, wc * mine_c)]
        send_note(1, inner + bends)
        pass_note(1)
        g_ab, g_ac, g_bb, g_bc, g_cc, e_ab, e_ac, e_bb, e_bc, e_cc = read_note(1, 10)
        finish_own(2)

        def form(aa, ab, ac, bb, bc, cc, u):
            a, b, c = u
            return (
                a * a * aa + b * b * bb + c * c * cc + 2.0 * (a * b * ab + a * c * ac + b * c * bc)
            )

        h = (curve_0, g_ab + e_ab, g_ac + e_ac, g_bb + e_bb, g_bc + e_bc, g_cc + e_cc)
        one = jnp.ones_like(norm_0)
        ratio_0 = g_bb / norm_0
        d1 = (ratio_0, one, 0.0 * one)
        step_1 = g_bb / form(*h, d1)
        mixing = step_1 * ratio_0 / step_0
        r2 = (-mixing, one + mixing, -step_1)
        norm_2 = form(norm_0, g_ab, g_ac, g_bb, g_bc, g_cc, r2)
        ratio_1 = norm_2 / g_bb
        d2 = tuple(r + ratio_1 * d for r, d in zip(r2, d1))
        step_2 = norm_2 / form(*h, d2)
        in_a = step_0 + step_1 * d1[0] + step_2 * d2[0]
        in_b = step_1 * d1[1] + step_2 * d2[1]
        in_c = step_1 * d1[2] + step_2 * d2[2]

        def write(k, carry):
            for half in range(halves):
                control[k, :, half * LANES : (half + 1) * LANES] = (
                    in_a * resid[0, k, half, own, :]
                    + in_b * second[k, half]
                    + in_c * resid[2, k, half, own, :]
                )
            return carry

        lax.fori_loop(0, members, write, 0)
        for level in range(levels):
            for half in range(halves):
                plane = level * halves + half
                a = full[0, plane, own, :]
                b = a - step_0 * full[1, plane, own, :]
                increment[level, :, half * LANES : (half + 1) * LANES] = (
                    in_a * a + in_b * b + in_c * full[2, plane, own, :]
                )

        for copy in (to_right, to_left, fields_right, fields_left):
            copy.wait_send()
        for turn in range(3):

            def settle(s, carry):
                chunk_copy(turn, s).wait_send()
                whole_copy(turn, s, me, lax.rem(me + s, groups)).wait_send()
                return carry

            lax.fori_loop(1, groups, settle, 0)
        for turn in range(2):

            def settle_edges(other, carry):
                for copy in edge_copies(turn, other, me, me):
                    copy.wait_send()
                return carry

            lax.fori_loop(0, groups, settle_edges, 0)

            def settle_notes(s, carry):
                note_copy(turn, s, me, lax.rem(me + s, groups)).wait_send()
                return carry

            lax.fori_loop(1, groups, settle_notes, 0)

            def settle_blocks(s, carry):
                sum_copy(turn, s, col, lax.rem(col + s, blocks)).wait_send()
                return carry

            lax.fori_loop(1, blocks, settle_blocks, 0)

    bf16 = jnp.bfloat16
    dma = pltpu.SemaphoreType.DMA
    scratch = [
        pltpu.VMEM((levels, members, width, depth), bf16),
        pltpu.VMEM((levels, members, HALO, depth), bf16),
        pltpu.VMEM((levels, members, HALO, depth), bf16),
        pltpu.VMEM((2, planes, rows, LANES), F32),
        pltpu.VMEM((planes, rows, LANES), F32),
        pltpu.VMEM((members, halves, rows, LANES), F32),
        pltpu.VMEM((3, members, halves, rows, LANES), F32),
        pltpu.VMEM((members, halves, width, LANES), F32),
        pltpu.VMEM((3, planes, width, LANES), F32),
        pltpu.VMEM((3, groups - 1, width, LANES), F32),
        pltpu.VMEM((3, planes, rows, LANES), F32),
        pltpu.VMEM((2, 1, LANES), F32),
        pltpu.VMEM((2, groups, 1, LANES), F32),
        pltpu.VMEM((2, 1, LANES), F32),
        pltpu.VMEM((2, blocks, 1, LANES), F32),
        dma,
        dma((2,)), dma((2,)), dma((2,)), dma((2,)),
        dma((3, groups - 1)), dma((3, groups - 1)), dma((3, groups - 1)), dma((3, groups - 1)),
        dma((2, groups)), dma((2, groups)), dma((2, groups)), dma((2, groups)),
        dma((2, groups - 1)), dma((2, groups - 1)), dma((2, blocks - 1)), dma((2, blocks - 1)),
    ]
    return kernel, scratch


def solution(mesh):
    groups, blocks = mesh.shape["mem"], mesh.shape["col"]

    def per_device(perturbations, loc_weights, offsets, obs_x, obs_y, obs_t, innovations, obs_rinv):
        levels, members, width, depth = perturbations.shape
        obs_rows = obs_x.shape[0] // LANES
        kernel, scratch = make_kernel(groups, blocks, levels, members, width, depth, obs_rows)
        vmem = pl.BlockSpec(memory_space=pltpu.VMEM)
        smem = pl.BlockSpec(memory_space=pltpu.SMEM)
        return pl.pallas_call(
            kernel,
            out_shape=(
                jax.ShapeDtypeStruct((members, width, depth), F32),
                jax.ShapeDtypeStruct((levels, width, depth), F32),
            ),
            in_specs=[pl.BlockSpec(memory_space=pl.ANY), smem, smem] + [vmem] * 5,
            out_specs=(vmem, vmem),
            scratch_shapes=scratch,
            compiler_params=pltpu.CompilerParams(collective_id=0, has_side_effects=True),
        )(
            perturbations, loc_weights, offsets.reshape(-1),
            *(v.reshape(obs_rows, LANES) for v in (obs_x, obs_y, obs_t, innovations, obs_rinv)),
        )

    return jax.shard_map(
        per_device,
        mesh=mesh,
        in_specs=(P(None, "mem", "col", None), P(), P()) + (P("col"),) * 5,
        out_specs=(P("mem", "col", None), P(None, "col", None)),
        check_vma=False,
    )
```

profile of v0, /device:TPU:1, one launch (start us, length us, event | category | flops | bytes accessed | tf_op | source)
XLA Modules:
  0.0 93.9 jit_solution(8659036583211482797)
XLA Ops:
  0.6 0.0 copy-start.1
  0.6 0.7 copy-done.1
  1.3 0.1 copy.11
  1.4 0.6 reshape.22.offsets
  2.0 89.3 %shard_map.95 = (f32[32,16,256]{2,1,0:T(8,128)}, f32[4,16,256]{2,1,0:T(8,128)}) custom-call(bf16[4,32,16,256]{3,2,1,0:T(8,128)(2,1)} %pert.1, f32[7]{0:T(128)} %weights.1, s32[14]{0:T(128)} %reshape.22.offsets, s32[16,128]{1,0:T(8,128)} %bitcast.5, s32[16,128]{1,0:T(8,128)} %bitcast.6, s32[16,128]{1,0:T(8,128)} %bitcast.7, f32[16,128]{1,0:T(8,128)} %bitcast.8, ...), custom_call_target="tpu_custom_call" | custom-call | tf_op jit(solution)/shard_map/pallas_call | solution.py:549
  91.3 0.0 copy-start
  91.3 1.9 %copy.14 = f32[32,16,256]{2,1,0:T(8,128)} copy(f32[32,16,256]{2,1,0:T(8,128)} %get-tuple-element.4) | data formatting | bytes 1048576
  93.2 0.0 copy-done
  93.2 0.6 copy.15
Async XLA Ops:
  0.6 0.7 copy-start.1
  91.3 1.9 %copy-start = (f32[4,16,256]{2,1,0:T(8,128)S(1)}, f32[4,16,256]{2,1,0:T(8,128)}, u32[]{:S(2)}) copy-start(f32[4,16,256]{2,1,0:T(8,128)} %get-tuple-element.5) | copy-start | bytes 196612
where the time goes:
time: 94 us; the launch traced here: 93.9 us
  Pallas kernels  89.3 us (95%)
  local copies, waits for them, and re-layouts  3.89 us (4%)
    pallas_call x1, Pallas kernels, per_device(): pl.pallas_call(kernel, out_shape=(jax.ShapeDtypeStruct((members, width, d...  89.3 us
    unnamed x7, local copies, waits for them, and re-layouts  3.3 us

commit v1 on v0

--- a/solution.py
+++ b/solution.py
@@ -10,6 +10,8 @@
 LANES = 128
 HALO = 2 * RADIUS
 F32 = jnp.float32
+UNROLL = 4
+TAP_UNROLL = 4
 MESH = pl.DeviceIdType.MESH
 
 
@@ -25,10 +27,10 @@
 
     def kernel(
         pert, weights, offsets, obs_x, obs_y, obs_t, innov, rinv,
-        control, increment,
+        out_a, out_b, out_c, inc_a, inc_b, inc_c, coefficients,
         p, p_low, p_high, fields, z, mixed, resid, second, part, gathered, full,
         note, group_note, sums, block_note,
-        load_sem, halo_send, halo_recv, field_send, field_recv,
+        load_sem, out_sem, mixed_send, mixed_recv, halo_send, halo_recv, field_send, field_recv,
         rs_send, rs_recv, ag_send, ag_recv, low_send, low_recv, high_send, high_recv,
         note_send, note_recv, sum_send, sum_recv,
     ):
@@ -95,8 +97,6 @@
                         level * width : (level + 1) * width, half * LANES : (half + 1) * LANES
                     ]
 
-        pl.semaphore_wait(barrier, groups - 1 + 2 * groups + blocks - 1)
-
         def remote(source, target, send, recv, device):
             return pltpu.make_async_remote_copy(
                 src_ref=source, dst_ref=target, send_sem=send, recv_sem=recv,
@@ -109,8 +109,6 @@
         to_left = remote(
             pert.at[:, :, pl.ds(0, HALO), :], p_high, halo_send.at[1], halo_recv.at[1], (me, left)
         )
-        to_right.start()
-        to_left.start()
         fields_right = remote(
             fields.at[:, :, last_own, :], fields.at[:, :, low_rows, :],
             field_send.at[0], field_recv.at[0], (me, right),
@@ -119,21 +117,18 @@
             fields.at[:, :, first_own, :], fields.at[:, :, high_rows, :],
             field_send.at[1], field_recv.at[1], (me, left),
         )
-        fields_right.start()
-        fields_left.start()
+        mixed_right = remote(
+            mixed.at[:, :, last_own, :], mixed.at[:, :, low_rows, :],
+            mixed_send.at[0], mixed_recv.at[0], (me, right),
+        )
+        mixed_left = remote(
+            mixed.at[:, :, first_own, :], mixed.at[:, :, high_rows, :],
+            mixed_send.at[1], mixed_recv.at[1], (me, left),
+        )
 
         tap_weight = [weights[s] for s in range(TAPS)]
-        along = [offsets[2 * s] for s in range(TAPS)]
-        across = [offsets[2 * s + 1] for s in range(TAPS)]
-
-        def shifted(pair, amount):
-            turn = jnp.where(amount < 0, amount + LANES, amount)
-            turned = [pltpu.roll(v, turn, 1) for v in pair]
-            spot = lax.broadcasted_iota(jnp.int32, pair[0].shape, 1) - amount
-            inside = (spot >= 0) & (spot < LANES)
-            return [
-                jnp.where(inside, turned[h], turned[1 - h]) for h in range(halves)
-            ]
+        along = [offsets[0, s] for s in range(TAPS)]
+        across = [offsets[1, s] for s in range(TAPS)]
 
         def mix(source, at, k):
             for half in range(halves):
@@ -147,56 +142,83 @@
 
         def mix_own():
             def step(k, carry):
-                for more in range(2):
-                    mix(p, own, 2 * k + more)
-                return carry
-
-            lax.fori_loop(0, members // 2, step, 0)
+                for more in range(UNROLL):
+                    mix(p, own, UNROLL * k + more)
+                return carry
+
+            lax.fori_loop(0, members // UNROLL, step, 0)
 
         def mix_edges():
             def step(k, carry):
-                for more in range(2):
-                    mix(p_low, low_rows, 2 * k + more)
-                    mix(p_high, high_rows, 2 * k + more)
-                return carry
-
-            lax.fori_loop(0, members // 2, step, 0)
+                for more in range(UNROLL):
+                    mix(p_low, low_rows, UNROLL * k + more)
+                    mix(p_high, high_rows, UNROLL * k + more)
+                return carry
+
+            lax.fori_loop(0, members // UNROLL, step, 0)
 
         reach = width + 2 * RADIUS
         row_at = lax.broadcasted_iota(jnp.int32, (reach, LANES), 0) + (col * width - RADIUS)
         keep = jnp.where((row_at >= 0) & (row_at < blocks * width), 1.0, 0.0)
 
+        def turns(amounts):
+            spots = [lax.broadcasted_iota(jnp.int32, (1, LANES), 1) - v for v in amounts]
+            return (
+                [jnp.where(v < 0, v + LANES, v) for v in amounts],
+                [(s >= 0) & (s < LANES) for s in spots],
+            )
+
+        back, forth = turns(across), turns([-v for v in across])
+
+        def stencil(source, starts, count, moves):
+            total = [None] * halves
+            for s in range(TAPS):
+                turned = [
+                    pltpu.roll(source(half, pl.ds(starts[s], count)), moves[0][s], 1)
+                    for half in range(halves)
+                ]
+                for half in range(halves):
+                    term = tap_weight[s] * jnp.where(
+                        moves[1][s], turned[half], turned[1 - half]
+                    )
+                    total[half] = term if total[half] is None else total[half] + term
+            return total
+
         def transpose_taps(turn):
+            starts = [RADIUS - v for v in along]
+
             def step(k, carry):
-                total = [jnp.zeros((reach, LANES), F32) for _ in range(halves)]
-                for s in range(TAPS):
-                    start = RADIUS - along[s]
-                    pair = [mixed[k, half, pl.ds(start, reach), :] for half in range(halves)]
-                    moved = shifted(pair, across[s])
-                    total = [total[half] + tap_weight[s] * moved[half] for half in range(halves)]
-                for half in range(halves):
-                    resid[turn, k, half, pl.ds(RADIUS, reach), :] = total[half] * keep
-                return carry
-
-            lax.fori_loop(0, members, step, 0)
+                for more in range(TAP_UNROLL):
+                    at = TAP_UNROLL * k + more
+                    total = stencil(lambda h, rows_at: mixed[at, h, rows_at, :], starts, reach, back)
+                    for half in range(halves):
+                        resid[turn, at, half, pl.ds(RADIUS, reach), :] = total[half] * keep
+                return carry
+
+            lax.fori_loop(0, members // TAP_UNROLL, step, 0)
 
         def taps_and_sum(turn):
-            def step(k, sums_so_far):
-                total = [jnp.zeros((width, LANES), F32) for _ in range(halves)]
-                for s in range(TAPS):
-                    start = HALO + along[s]
-                    pair = [resid[turn, k, half, pl.ds(start, width), :] for half in range(halves)]
-                    moved = shifted(pair, -across[s])
-                    total = [total[half] + tap_weight[s] * moved[half] for half in range(halves)]
-                return tuple(
-                    sums_so_far[level * halves + half]
-                    + p[level, k, :, half * LANES : (half + 1) * LANES].astype(F32) * total[half]
-                    for level in range(levels)
-                    for half in range(halves)
-                )
+            starts = [HALO + v for v in along]
+
+            def step(k, so_far):
+                for more in range(TAP_UNROLL):
+                    at = TAP_UNROLL * k + more
+                    total = stencil(
+                        lambda h, rows_at: resid[turn, at, h, rows_at, :], starts, width, forth
+                    )
+                    so_far = tuple(
+                        so_far[level * halves + half]
+                        + p[level, at, :, half * LANES : (half + 1) * LANES].astype(F32) * total[half]
+                        for level in range(levels)
+                        for half in range(halves)
+                    )
+                return so_far
 
             summed = lax.fori_loop(
-                0, members, step, tuple(jnp.zeros((width, LANES), F32) for _ in range(planes))
+                0,
+                members // TAP_UNROLL,
+                step,
+                tuple(jnp.zeros((width, LANES), F32) for _ in range(planes)),
             )
             for plane in range(planes):
                 part[turn, plane] = summed[plane]
@@ -258,11 +280,6 @@
             return total
 
         def start_spread(turn, edges):
-            def step(s, carry):
-                whole_copy(turn, s, me, lax.rem(me + s, groups)).start()
-                return carry
-
-            lax.fori_loop(1, groups, step, 0)
             if edges:
 
                 def edge_step(other, carry):
@@ -271,6 +288,12 @@
                     return carry
 
                 lax.fori_loop(0, groups, edge_step, 0)
+
+            def step(s, carry):
+                whole_copy(turn, s, me, lax.rem(me + s, groups)).start()
+                return carry
+
+            lax.fori_loop(1, groups, step, 0)
 
         def finish_own(turn):
             def step(s, carry):
@@ -335,12 +358,72 @@
                 for at in range(count)
             ]
 
+        def out_copies(which):
+            source = (resid.at[0, :, :, own, :], second, resid.at[2, :, :, own, :])[which]
+            target = (out_a, out_b, out_c)[which]
+            return [
+                pltpu.make_async_copy(
+                    source.at[:, half],
+                    target.at[:, :, pl.ds(half * LANES, LANES)],
+                    out_sem.at[which, half],
+                )
+                for half in range(halves)
+            ]
+
+        def store_out(which):
+            for copy in out_copies(which):
+                copy.start()
+
         def all_of(value):
             return jnp.sum(jnp.sum(value, axis=0, keepdims=True), axis=1, keepdims=True)
 
         load.wait()
         for plane in range(planes):
             z[plane, own, :] = fields[0, plane, own, :]
+        mix_own()
+        pl.semaphore_wait(barrier, groups - 1 + 2 * groups + blocks - 1)
+        mixed_right.start()
+        mixed_left.start()
+        mixed_right.wait_recv()
+        mixed_left.wait_recv()
+        for copy in (fields_right, fields_left, to_right, to_left):
+            copy.start()
+
+        @pl.when(col == 0)
+        def _():
+            mixed[:, :, low_rows, :] = jnp.zeros((members, halves, HALO, LANES), F32)
+
+        @pl.when(col == blocks - 1)
+        def _():
+            mixed[:, :, high_rows, :] = jnp.zeros((members, halves, HALO, LANES), F32)
+
+        transpose_taps(0)
+        taps_and_sum(0)
+        start_sums(0)
+        store_out(0)
+
+        def square(k, total):
+            for half in range(halves):
+                value = resid[0, k, half, own, :]
+                total = total + value * value
+            return total
+
+        norm = all_of(lax.fori_loop(0, members, square, jnp.zeros((width, LANES), F32)))
+        mine = finish_sums(0)
+        start_spread(0, True)
+        send_note(0, [norm, all_of(fields[1, me, own, :] * mine * mine)])
+        finish_own(0)
+        pass_note(0)
+
+        def image_of_first(at):
+            for plane in range(planes):
+                z[plane, at, :] = (
+                    fields[0, plane, at, :] + fields[1, plane, at, :] * full[0, plane, at, :]
+                )
+
+        mixed_right.wait_send()
+        mixed_left.wait_send()
+        image_of_first(own)
         mix_own()
         fields_right.wait_recv()
         fields_left.wait_recv()
@@ -350,38 +433,9 @@
             for plane in range(planes):
                 fields[which, plane, low_rows, :] = fields[which, plane, low_rows, :] * has_left
                 fields[which, plane, high_rows, :] = fields[which, plane, high_rows, :] * has_right
-        for plane in range(planes):
-            z[plane, low_rows, :] = fields[0, plane, low_rows, :]
-            z[plane, high_rows, :] = fields[0, plane, high_rows, :]
+        finish_edges(0)
         to_right.wait_recv()
         to_left.wait_recv()
-        mix_edges()
-        transpose_taps(0)
-        taps_and_sum(0)
-        start_sums(0)
-
-        def square(k, total):
-            for half in range(halves):
-                value = resid[0, k, half, own, :]
-                total = total + value * value
-            return total
-
-        norm = all_of(lax.fori_loop(0, members, square, jnp.zeros((width, LANES), F32)))
-        mine = finish_sums(0)
-        start_spread(0, True)
-        send_note(0, [norm, all_of(fields[1, me, own, :] * mine * mine)])
-        finish_own(0)
-        pass_note(0)
-
-        def image_of_first(at):
-            for plane in range(planes):
-                z[plane, at, :] = (
-                    fields[0, plane, at, :] + fields[1, plane, at, :] * full[0, plane, at, :]
-                )
-
-        image_of_first(own)
-        mix_own()
-        finish_edges(0)
         image_of_first(low_rows)
         image_of_first(high_rows)
         mix_edges()
@@ -410,6 +464,7 @@
         transpose_taps(2)
         taps_and_sum(2)
         start_sums(2)
+        store_out(2)
 
         def products(k, so_far):
             ab, ac, bb, bc, cc = so_far
@@ -427,6 +482,7 @@
                 0, members, products, tuple(jnp.zeros((width, LANES), F32) for _ in range(5))
             )
         ]
+        store_out(1)
         mine_c = finish_sums(2)
         start_spread(2, False)
         mine_a = full[0, me, own, :]
@@ -460,27 +516,22 @@
         in_b = step_1 * d1[1] + step_2 * d2[1]
         in_c = step_1 * d1[2] + step_2 * d2[2]
 
-        def write(k, carry):
-            for half in range(halves):
-                control[k, :, half * LANES : (half + 1) * LANES] = (
-                    in_a * resid[0, k, half, own, :]
-                    + in_b * second[k, half]
-                    + in_c * resid[2, k, half, own, :]
-                )
-            return carry
-
-        lax.fori_loop(0, members, write, 0)
+        for at, value in enumerate((in_a, in_b, in_c)):
+            coefficients[pl.ds(at, 1), :] = jnp.broadcast_to(value, (1, depth))
         for level in range(levels):
             for half in range(halves):
                 plane = level * halves + half
+                at = (level, slice(None), slice(half * LANES, (half + 1) * LANES))
                 a = full[0, plane, own, :]
-                b = a - step_0 * full[1, plane, own, :]
-                increment[level, :, half * LANES : (half + 1) * LANES] = (
-                    in_a * a + in_b * b + in_c * full[2, plane, own, :]
-                )
+                inc_a[at] = a
+                inc_b[at] = a - step_0 * full[1, plane, own, :]
+                inc_c[at] = full[2, plane, own, :]
 
         for copy in (to_right, to_left, fields_right, fields_left):
             copy.wait_send()
+        for which in range(3):
+            for copy in out_copies(which):
+                copy.wait()
         for turn in range(3):
 
             def settle(s, carry):
@@ -529,7 +580,7 @@
         pltpu.VMEM((2, 1, LANES), F32),
         pltpu.VMEM((2, blocks, 1, LANES), F32),
         dma,
-        dma((2,)), dma((2,)), dma((2,)), dma((2,)),
+        dma((3, halves)), dma((2,)), dma((2,)), dma((2,)), dma((2,)), dma((2,)), dma((2,)),
         dma((3, groups - 1)), dma((3, groups - 1)), dma((3, groups - 1)), dma((3, groups - 1)),
         dma((2, groups)), dma((2, groups)), dma((2, groups)), dma((2, groups)),
         dma((2, groups - 1)), dma((2, groups - 1)), dma((2, blocks - 1)), dma((2, blocks - 1)),
@@ -546,19 +597,23 @@
         kernel, scratch = make_kernel(groups, blocks, levels, members, width, depth, obs_rows)
         vmem = pl.BlockSpec(memory_space=pltpu.VMEM)
         smem = pl.BlockSpec(memory_space=pltpu.SMEM)
-        return pl.pallas_call(
+        hbm = pl.BlockSpec(memory_space=pl.ANY)
+        a, b, c, inc_a, inc_b, inc_c, factors = pl.pallas_call(
             kernel,
-            out_shape=(
-                jax.ShapeDtypeStruct((members, width, depth), F32),
-                jax.ShapeDtypeStruct((levels, width, depth), F32),
-            ),
-            in_specs=[pl.BlockSpec(memory_space=pl.ANY), smem, smem] + [vmem] * 5,
-            out_specs=(vmem, vmem),
+            out_shape=(jax.ShapeDtypeStruct((members, width, depth), F32),) * 3
+            + (jax.ShapeDtypeStruct((levels, width, depth), F32),) * 3
+            + (jax.ShapeDtypeStruct((3, depth), F32),),
+            in_specs=[hbm, smem, smem] + [vmem] * 5,
+            out_specs=(hbm,) * 3 + (vmem,) * 4,
             scratch_shapes=scratch,
             compiler_params=pltpu.CompilerParams(collective_id=0, has_side_effects=True),
         )(
-            perturbations, loc_weights, offsets.reshape(-1),
+            perturbations, loc_weights, offsets.T,
             *(v.reshape(obs_rows, LANES) for v in (obs_x, obs_y, obs_t, innovations, obs_rinv)),
+        )
+        return (
+            factors[0] * a + factors[1] * b + factors[2] * c,
+            factors[0] * inc_a + factors[1] * inc_b + factors[2] * inc_c,
         )
 
     return jax.shard_map(

time: 94 us -> 83.8 us (0.89)
  Pallas kernels: 89.3 us -> 78.2 us
  other arithmetic: 0 us -> 3.87 us
  local copies, waits for them, and re-layouts: 3.89 us -> 0.8 us
    pallas_call x1, Pallas kernels: 89.3 us -> 78.2 us  [per_device(): pl.pallas_call(kernel, out_shape=(jax.ShapeDtypeStruct((members, width, d...]
    add x0 -> x2, other arithmetic: none -> 3.87 us  [the longest x1 2.32 us: per_device(): factors[0] * a + factors[1] * b + factors[2] * c]
    unnamed x7 -> x0, local copies, waits for them, and re-layouts: 3.3 us -> none
where the time goes in v1:
time: 83.8 us; the launch traced here: 83.5 us
  Pallas kernels  78.2 us (93%)
  other arithmetic  3.87 us (5%)
    pallas_call x1, Pallas kernels, per_device(): pl.pallas_call(kernel, out_shape=(jax.ShapeDtypeStruct((members, width, d...  78.2 us
    add x1, other arithmetic, per_device(): factors[0] * a + factors[1] * b + factors[2] * c  2.32 us

profile of v1, /device:TPU:1, one launch (start us, length us, event | category | flops | bytes accessed | tf_op | source)
XLA Modules:
  0.0 83.5 jit_solution(2854053982724587779)
XLA Ops:
  0.6 78.2 %shard_map.95 = (f32[32,16,256]{2,1,0:T(8,128)}, f32[32,16,256]{2,1,0:T(8,128)}, f32[32,16,256]{2,1,0:T(8,128)}, f32[4,16,256]{2,1,0:T(8,128)}, f32[4,16,256]{2,...) custom-call(bf16[4,32,16,256]{3,2,1,0:T(8,128)(2,1)} %pert.1, f32[7]{0:T(128)} %weights.1, s32[2,7]{1,0:T(2,128)} %bitcast.20, ...), custom_call_target="tpu_custom_call" | custom-call | tf_op jit(solution)/shard_map/pallas_call | solution.py:601
  78.9 0.8 fusion
  79.7 1.5 %multiply_add_fusion.1 = f32[4,16,256]{2,1,0:T(8,128)} fusion(f32[4,16,256]{2,1,0:T(8,128)} %get-tuple-element.15, f32[4,16,256]{2,1,0:T(8,128)} %get-tuple-element.14, f32[4,16,256]{2,1,0:T(8,128)} %get-tuple-element.13, f32[256]{0:T(256)S(1)} %bitcast.11, f32[256]{0:T(256)S(1)} %bitcast.13, f32[256]{0:T(256)S(1)} %bitcast.9), kind=kLoop, calls=%fused_computation.1 | loop fusion | flops 81920 | bytes 265216 | tf_op jit(solution)/shard_map/add | solution.py:616
  81.2 2.3 %multiply_add_fusion = f32[32,16,256]{2,1,0:T(8,128)} fusion(f32[32,16,256]{2,1,0:T(8,128)} %get-tuple-element.12, f32[32,16,256]{2,1,0:T(8,128)} %get-tuple-element.11, f32[32,16,256]{2,1,0:T(8,128)} %get-tuple-element.10, f32[256]{0:T(256)S(1)} %bitcast.12, f32[256]{0:T(256)S(1)} %bitcast.14, f32[256]{0:T(256)S(1)} %bitcast.10), kind=kLoop, calls=%fused_computation | loop fusion | flops 655360 | bytes 2100224 | tf_op jit(solution)/shard_map/add | solution.py:615

commit v2 on v1

--- a/solution.py
+++ b/solution.py
@@ -27,10 +27,10 @@
 
     def kernel(
         pert, weights, offsets, obs_x, obs_y, obs_t, innov, rinv,
-        out_a, out_b, out_c, inc_a, inc_b, inc_c, coefficients,
+        control, increment,
         p, p_low, p_high, fields, z, mixed, resid, second, part, gathered, full,
         note, group_note, sums, block_note,
-        load_sem, out_sem, mixed_send, mixed_recv, halo_send, halo_recv, field_send, field_recv,
+        hello, load_sem, mixed_send, mixed_recv, halo_send, halo_recv, field_send, field_recv,
         rs_send, rs_recv, ag_send, ag_recv, low_send, low_recv, high_send, high_recv,
         note_send, note_recv, sum_send, sum_recv,
     ):
@@ -48,15 +48,21 @@
         load.start()
         for step in range(1, groups):
             greet((lax.rem(me + step, groups), col))
-        for other in range(groups):
-            greet((other, right))
-            greet((other, left))
-
-        def greet_block(step, carry):
-            greet((me, lax.rem(col + step, blocks)))
-            return carry
-
-        lax.fori_loop(1, blocks, greet_block, 0)
+        greet((me, right))
+        greet((me, left))
+
+        def hello_peers(turn):
+            away = 1 << turn
+            return lax.rem(col + away, blocks), lax.rem(col + blocks - away, blocks)
+
+        def say_hello(turn):
+            up, down = hello_peers(turn)
+            pl.semaphore_signal(hello.at[turn, 0], inc=1, device_id=(me, up), device_id_type=MESH)
+            pl.semaphore_signal(hello.at[turn, 1], inc=1, device_id=(me, down), device_id_type=MESH)
+
+        def hear_hello(turn):
+            pl.semaphore_wait(hello.at[turn, 0], 1)
+            pl.semaphore_wait(hello.at[turn, 1], 1)
 
         lanes8 = lax.broadcasted_iota(jnp.int32, (1, LANES), 1)
         cell_rows = lax.broadcasted_iota(jnp.int32, (levels * width, LANES), 0)
@@ -358,22 +364,6 @@
                 for at in range(count)
             ]
 
-        def out_copies(which):
-            source = (resid.at[0, :, :, own, :], second, resid.at[2, :, :, own, :])[which]
-            target = (out_a, out_b, out_c)[which]
-            return [
-                pltpu.make_async_copy(
-                    source.at[:, half],
-                    target.at[:, :, pl.ds(half * LANES, LANES)],
-                    out_sem.at[which, half],
-                )
-                for half in range(halves)
-            ]
-
-        def store_out(which):
-            for copy in out_copies(which):
-                copy.start()
-
         def all_of(value):
             return jnp.sum(jnp.sum(value, axis=0, keepdims=True), axis=1, keepdims=True)
 
@@ -381,13 +371,16 @@
         for plane in range(planes):
             z[plane, own, :] = fields[0, plane, own, :]
         mix_own()
-        pl.semaphore_wait(barrier, groups - 1 + 2 * groups + blocks - 1)
+        pl.semaphore_wait(barrier, groups - 1 + 2)
         mixed_right.start()
         mixed_left.start()
+        for copy in (fields_right, fields_left, to_right, to_left):
+            copy.start()
+        say_hello(0)
         mixed_right.wait_recv()
         mixed_left.wait_recv()
-        for copy in (fields_right, fields_left, to_right, to_left):
-            copy.start()
+        hear_hello(0)
+        say_hello(1)
 
         @pl.when(col == 0)
         def _():
@@ -398,9 +391,10 @@
             mixed[:, :, high_rows, :] = jnp.zeros((members, halves, HALO, LANES), F32)
 
         transpose_taps(0)
+        hear_hello(1)
+        say_hello(2)
         taps_and_sum(0)
         start_sums(0)
-        store_out(0)
 
         def square(k, total):
             for half in range(halves):
@@ -410,9 +404,12 @@
 
         norm = all_of(lax.fori_loop(0, members, square, jnp.zeros((width, LANES), F32)))
         mine = finish_sums(0)
+        hear_hello(2)
+        say_hello(3)
         start_spread(0, True)
         send_note(0, [norm, all_of(fields[1, me, own, :] * mine * mine)])
         finish_own(0)
+        hear_hello(3)
         pass_note(0)
 
         def image_of_first(at):
@@ -464,7 +461,6 @@
         transpose_taps(2)
         taps_and_sum(2)
         start_sums(2)
-        store_out(2)
 
         def products(k, so_far):
             ab, ac, bb, bc, cc = so_far
@@ -482,7 +478,6 @@
                 0, members, products, tuple(jnp.zeros((width, LANES), F32) for _ in range(5))
             )
         ]
-        store_out(1)
         mine_c = finish_sums(2)
         start_spread(2, False)
         mine_a = full[0, me, own, :]
@@ -516,22 +511,29 @@
         in_b = step_1 * d1[1] + step_2 * d2[1]
         in_c = step_1 * d1[2] + step_2 * d2[2]
 
-        for at, value in enumerate((in_a, in_b, in_c)):
-            coefficients[pl.ds(at, 1), :] = jnp.broadcast_to(value, (1, depth))
+        def write(step, carry):
+            for more in range(UNROLL):
+                k = UNROLL * step + more
+                for half in range(halves):
+                    control[k, :, half * LANES : (half + 1) * LANES] = (
+                        in_a * resid[0, k, half, own, :]
+                        + in_b * second[k, half]
+                        + in_c * resid[2, k, half, own, :]
+                    )
+            return carry
+
+        lax.fori_loop(0, members // UNROLL, write, 0)
         for level in range(levels):
             for half in range(halves):
                 plane = level * halves + half
-                at = (level, slice(None), slice(half * LANES, (half + 1) * LANES))
                 a = full[0, plane, own, :]
-                inc_a[at] = a
-                inc_b[at] = a - step_0 * full[1, plane, own, :]
-                inc_c[at] = full[2, plane, own, :]
+                b = a - step_0 * full[1, plane, own, :]
+                increment[level, :, half * LANES : (half + 1) * LANES] = (
+                    in_a * a + in_b * b + in_c * full[2, plane, own, :]
+                )
 
         for copy in (to_right, to_left, fields_right, fields_left):
             copy.wait_send()
-        for which in range(3):
-            for copy in out_copies(which):
-                copy.wait()
         for turn in range(3):
 
             def settle(s, carry):
@@ -579,8 +581,9 @@
         pltpu.VMEM((2, groups, 1, LANES), F32),
         pltpu.VMEM((2, 1, LANES), F32),
         pltpu.VMEM((2, blocks, 1, LANES), F32),
+        pltpu.SemaphoreType.REGULAR((4, 2)),
         dma,
-        dma((3, halves)), dma((2,)), dma((2,)), dma((2,)), dma((2,)), dma((2,)), dma((2,)),
+        dma((2,)), dma((2,)), dma((2,)), dma((2,)), dma((2,)), dma((2,)),
         dma((3, groups - 1)), dma((3, groups - 1)), dma((3, groups - 1)), dma((3, groups - 1)),
         dma((2, groups)), dma((2, groups)), dma((2, groups)), dma((2, groups)),
         dma((2, groups - 1)), dma((2, groups - 1)), dma((2, blocks - 1)), dma((2, blocks - 1)),
@@ -598,22 +601,19 @@
         vmem = pl.BlockSpec(memory_space=pltpu.VMEM)
         smem = pl.BlockSpec(memory_space=pltpu.SMEM)
         hbm = pl.BlockSpec(memory_space=pl.ANY)
-        a, b, c, inc_a, inc_b, inc_c, factors = pl.pallas_call(
+        return pl.pallas_call(
             kernel,
-            out_shape=(jax.ShapeDtypeStruct((members, width, depth), F32),) * 3
-            + (jax.ShapeDtypeStruct((levels, width, depth), F32),) * 3
-            + (jax.ShapeDtypeStruct((3, depth), F32),),
+            out_shape=(
+                pltpu.VMEM((members, width, depth), F32),
+                pltpu.VMEM((levels, width, depth), F32),
+            ),
             in_specs=[hbm, smem, smem] + [vmem] * 5,
-            out_specs=(hbm,) * 3 + (vmem,) * 4,
+            out_specs=(vmem,) * 2,
             scratch_shapes=scratch,
             compiler_params=pltpu.CompilerParams(collective_id=0, has_side_effects=True),
         )(
             perturbations, loc_weights, offsets.T,
             *(v.reshape(obs_rows, LANES) for v in (obs_x, obs_y, obs_t, innovations, obs_rinv)),
-        )
-        return (
-            factors[0] * a + factors[1] * b + factors[2] * c,
-            factors[0] * inc_a + factors[1] * inc_b + factors[2] * inc_c,
         )
 
     return jax.shard_map(

time: 83.8 us -> 76.7 us (0.915)
  other arithmetic: 3.87 us -> 0 us
  Pallas kernels: 78.2 us -> 74.5 us
    add x2 -> x0, other arithmetic: 3.87 us -> none  [the longest x1 2.32 us: per_device(): factors[0] * a + factors[1] * b + factors[2] * c]
    pallas_call x1, Pallas kernels: 78.2 us -> 74.5 us  [per_device(): pl.pallas_call(kernel, out_shape=(pltpu.VMEM((members, width, depth), F32...]
    unnamed x0 -> x2, local copies, waits for them, and re-layouts: none -> 1.42 us
where the time goes in v2:
time: 76.7 us; the launch traced here: 76.6 us
  Pallas kernels  74.5 us (97%)
  local copies, waits for them, and re-layouts  1.42 us (2%)
    pallas_call x1, Pallas kernels, per_device(): pl.pallas_call(kernel, out_shape=(pltpu.VMEM((members, width, depth), F32...  74.5 us

profile of v2, /device:TPU:1, one launch (start us, length us, event | category | flops | bytes accessed | tf_op | source)
XLA Modules:
  0.0 76.6 jit_solution(14346395430585624034)
XLA Ops:
  0.6 74.5 %shard_map.95 = (f32[32,16,256]{2,1,0:T(8,128)S(1)}, f32[4,16,256]{2,1,0:T(8,128)S(1)}) custom-call(bf16[4,32,16,256]{3,2,1,0:T(8,128)(2,1)} %pert.1, f32[7]{0:T(128)} %weights.1, s32[2,7]{1,0:T(2,128)} %bitcast.11, s32[16,128]{1,0:T(8,128)} %bitcast.6, s32[16,128]{1,0:T(8,128)} %bitcast.7, s32[16,128]{1,0:T(8,128)} %bitcast.8, f32[16,128]{1,0:T(8,128)} %bitcast.9, ...), custom_call_target="tpu_custom_call" | custom-call | tf_op jit(solution)/shard_map/pallas_call | solution.py:604
  75.1 0.8 %copy.12 = f32[32,16,256]{2,1,0:T(8,128)} copy(f32[32,16,256]{2,1,0:T(8,128)S(1)} %get-tuple-element.2) | data formatting | bytes 1048576
  75.9 0.6 copy.13

commit v3 on v2

--- a/solution.py
+++ b/solution.py
@@ -26,8 +26,9 @@
     first_own = pl.ds(HALO, HALO)
 
     def kernel(
-        pert, weights, offsets, obs_x, obs_y, obs_t, innov, rinv,
+        pert, weights_in, offsets_in, obs_x_in, obs_y_in, obs_t_in, innov_in, rinv_in,
         control, increment,
+        weights, offsets, obs_x, obs_y, obs_t, innov, rinv,
         p, p_low, p_high, fields, z, mixed, resid, second, part, gathered, full,
         note, group_note, sums, block_note,
         hello, load_sem, mixed_send, mixed_recv, halo_send, halo_recv, field_send, field_recv,
@@ -36,33 +37,69 @@
     ):
         me = lax.axis_index("mem")
         col = lax.axis_index("col")
-        right = lax.rem(col + 1, blocks)
-        left = lax.rem(col + blocks - 1, blocks)
+        right, left = col + 1, col - 1
+        has_left, has_right = col > 0, col < blocks - 1
 
         barrier = pltpu.get_barrier_semaphore()
 
         def greet(target):
             pl.semaphore_signal(barrier, inc=1, device_id=target, device_id_type=MESH)
 
-        load = pltpu.make_async_copy(pert, p, load_sem)
+        loads = [
+            pltpu.make_async_copy(source, target, load_sem.at[at])
+            for at, (source, target) in enumerate(
+                (
+                    (obs_x_in, obs_x), (obs_y_in, obs_y), (obs_t_in, obs_t), (innov_in, innov),
+                    (rinv_in, rinv), (weights_in, weights), (offsets_in, offsets), (pert, p),
+                )
+            )
+        ]
+        load = loads.pop()
+        for copy in loads:
+            copy.start()
         load.start()
         for step in range(1, groups):
             greet((lax.rem(me + step, groups), col))
-        greet((me, right))
-        greet((me, left))
-
-        def hello_peers(turn):
+
+        @pl.when(has_right)
+        def _():
+            greet((me, right))
+
+        @pl.when(has_left)
+        def _():
+            greet((me, left))
+
+        def hello_sides(turn):
             away = 1 << turn
-            return lax.rem(col + away, blocks), lax.rem(col + blocks - away, blocks)
+            return (0, col + away, col + away < blocks), (1, col - away, col >= away)
 
         def say_hello(turn):
-            up, down = hello_peers(turn)
-            pl.semaphore_signal(hello.at[turn, 0], inc=1, device_id=(me, up), device_id_type=MESH)
-            pl.semaphore_signal(hello.at[turn, 1], inc=1, device_id=(me, down), device_id_type=MESH)
+            for side, peer, there in hello_sides(turn):
+
+                @pl.when(there)
+                def _():
+                    pl.semaphore_signal(
+                        hello.at[turn, side], inc=1, device_id=(me, peer), device_id_type=MESH
+                    )
 
         def hear_hello(turn):
-            pl.semaphore_wait(hello.at[turn, 0], 1)
-            pl.semaphore_wait(hello.at[turn, 1], 1)
+            for side, _, there in hello_sides(turn):
+
+                @pl.when(there)
+                def _():
+                    pl.semaphore_wait(hello.at[turn, 1 - side], 1)
+
+        @pl.when(col == 0)
+        def _():
+            p_low[...] = jnp.zeros(p_low.shape, p_low.dtype)
+            fields[:, :, low_rows, :] = jnp.zeros((2, planes, HALO, LANES), F32)
+            full[:, :, low_rows, :] = jnp.zeros((3, planes, HALO, LANES), F32)
+
+        @pl.when(col == blocks - 1)
+        def _():
+            p_high[...] = jnp.zeros(p_high.shape, p_high.dtype)
+            fields[:, :, high_rows, :] = jnp.zeros((2, planes, HALO, LANES), F32)
+            full[:, :, high_rows, :] = jnp.zeros((3, planes, HALO, LANES), F32)
 
         lanes8 = lax.broadcasted_iota(jnp.int32, (1, LANES), 1)
         cell_rows = lax.broadcasted_iota(jnp.int32, (levels * width, LANES), 0)
@@ -86,6 +123,8 @@
                 left_side, right_side, (((1,), (1,)), ((), ())), preferred_element_type=F32
             )
 
+        for copy in loads:
+            copy.wait()
         spread = lax.fori_loop(
             0, obs_rows, place, jnp.zeros((6 * levels * width, depth), F32)
         )
@@ -109,12 +148,32 @@
                 device_id=device, device_id_type=MESH,
             )
 
-        to_right = remote(
-            pert.at[:, :, pl.ds(width - HALO, HALO), :], p_low, halo_send.at[0], halo_recv.at[0], (me, right)
-        )
-        to_left = remote(
-            pert.at[:, :, pl.ds(0, HALO), :], p_high, halo_send.at[1], halo_recv.at[1], (me, left)
-        )
+        to_right = [
+            remote(
+                pert.at[level, :, pl.ds(width - HALO, HALO), :], p_low.at[level],
+                halo_send.at[0, level], halo_recv.at[0, level], (me, right),
+            )
+            for level in range(levels)
+        ]
+        to_left = [
+            remote(
+                pert.at[level, :, pl.ds(0, HALO), :], p_high.at[level],
+                halo_send.at[1, level], halo_recv.at[1, level], (me, left),
+            )
+            for level in range(levels)
+        ]
+
+        def send_halo(*which):
+            @pl.when(has_right)
+            def _():
+                for level in which:
+                    to_right[level].start()
+
+            @pl.when(has_left)
+            def _():
+                for level in which:
+                    to_left[level].start()
+
         fields_right = remote(
             fields.at[:, :, last_own, :], fields.at[:, :, low_rows, :],
             field_send.at[0], field_recv.at[0], (me, right),
@@ -229,93 +288,63 @@
             for plane in range(planes):
                 part[turn, plane] = summed[plane]
 
-        def chunk_copy(turn, step):
-            peer = lax.rem(me + step, groups)
-            return remote(
-                part.at[turn, peer], gathered.at[turn, step - 1],
-                rs_send.at[turn, step - 1], rs_recv.at[turn, step - 1], (peer, col),
-            )
-
-        def whole_copy(turn, step, sender, peer):
-            spot = full.at[turn, sender, own, :]
-            return remote(
-                spot, spot, ag_send.at[turn, step - 1], ag_recv.at[turn, step - 1], (peer, col)
-            )
-
-        def edge_copies(turn, other, sender, slot):
-            return (
+        def wait_bytes(ref, sem):
+            pltpu.make_async_copy(ref, ref, sem).wait()
+
+        def start_sums(turn):
+            for step in range(1, groups):
+                peer = lax.rem(me + step, groups)
                 remote(
-                    full.at[turn, sender, last_own, :], full.at[turn, sender, low_rows, :],
-                    low_send.at[turn, other], low_recv.at[turn, slot], (other, right),
-                ),
-                remote(
-                    full.at[turn, sender, first_own, :], full.at[turn, sender, high_rows, :],
-                    high_send.at[turn, other], high_recv.at[turn, slot], (other, left),
-                ),
-            )
-
-        def note_copy(which, step, sender, peer):
-            return remote(
-                note.at[which], group_note.at[which, sender],
-                note_send.at[which, step - 1], note_recv.at[which, step - 1], (peer, col),
-            )
-
-        def sum_copy(which, step, sender, peer):
-            return remote(
-                sums.at[which], block_note.at[which, sender],
-                sum_send.at[which, step - 1], sum_recv.at[which, step - 1], (me, peer),
-            )
-
-        def start_sums(turn):
-            def step(s, carry):
-                chunk_copy(turn, s).start()
-                return carry
-
-            lax.fori_loop(1, groups, step, 0)
+                    part.at[turn, peer], gathered.at[turn, step - 1],
+                    rs_send.at[turn], rs_recv.at[turn], (peer, col),
+                ).start()
 
         def finish_sums(turn):
-            def step(s, carry):
-                chunk_copy(turn, s).wait_recv()
-                return carry
-
-            lax.fori_loop(1, groups, step, 0)
+            wait_bytes(gathered.at[turn], rs_recv.at[turn])
             total = part[turn, me]
             for s in range(groups - 1):
                 total = total + gathered[turn, s]
             full[turn, me, own, :] = total
             return total
 
-        def start_spread(turn, edges):
-            if edges:
-
-                def edge_step(other, carry):
-                    for copy in edge_copies(turn, other, me, me):
-                        copy.start()
-                    return carry
-
-                lax.fori_loop(0, groups, edge_step, 0)
-
-            def step(s, carry):
-                whole_copy(turn, s, me, lax.rem(me + s, groups)).start()
-                return carry
-
-            lax.fori_loop(1, groups, step, 0)
+        def start_edges(turn):
+            @pl.when(has_right)
+            def _():
+                for step in range(groups):
+                    remote(
+                        full.at[turn, me, last_own, :], full.at[turn, me, low_rows, :],
+                        low_send.at[turn], low_recv.at[turn], (lax.rem(me + step, groups), right),
+                    ).start()
+
+            @pl.when(has_left)
+            def _():
+                for step in range(groups):
+                    remote(
+                        full.at[turn, me, first_own, :], full.at[turn, me, high_rows, :],
+                        high_send.at[turn], high_recv.at[turn], (lax.rem(me + step, groups), left),
+                    ).start()
+
+        def start_group(turn):
+            spot = full.at[turn, me, own, :]
+            for step in range(1, groups):
+                remote(
+                    spot, spot, ag_send.at[turn], ag_recv.at[turn], (lax.rem(me + step, groups), col)
+                ).start()
+
+        def others(turn):
+            return full.at[turn, pl.ds(0, groups - 1), own, :]
 
         def finish_own(turn):
-            def step(s, carry):
-                peer = lax.rem(me + groups - s, groups)
-                whole_copy(turn, s, peer, peer).wait_recv()
-                return carry
-
-            lax.fori_loop(1, groups, step, 0)
+            wait_bytes(others(turn), ag_recv.at[turn])
 
         def finish_edges(turn):
-            def step(other, carry):
-                for copy in edge_copies(turn, other, other, other):
-                    copy.wait_recv()
-                return carry
-
-            lax.fori_loop(0, groups, step, 0)
+            @pl.when(has_left)
+            def _():
+                wait_bytes(full.at[turn, :, low_rows, :], low_recv.at[turn])
+
+            @pl.when(has_right)
+            def _():
+                wait_bytes(full.at[turn, :, high_rows, :], high_recv.at[turn])
 
         def send_note(which, values):
             row = jnp.zeros((1, LANES), F32)
@@ -323,39 +352,27 @@
                 row = jnp.where(lanes8 == at, value, row)
             note[which] = row
             group_note[which, me] = row
-
-            def step(s, carry):
-                note_copy(which, s, me, lax.rem(me + s, groups)).start()
-                return carry
-
-            lax.fori_loop(1, groups, step, 0)
+            for step in range(1, groups):
+                remote(
+                    note.at[which], group_note.at[which, me],
+                    note_send.at[which], note_recv.at[which], (lax.rem(me + step, groups), col),
+                ).start()
 
         def pass_note(which):
-            def step(s, carry):
-                peer = lax.rem(me + groups - s, groups)
-                note_copy(which, s, peer, peer).wait_recv()
-                return carry
-
-            lax.fori_loop(1, groups, step, 0)
+            wait_bytes(group_note.at[which, pl.ds(0, groups - 1)], note_recv.at[which])
             total = group_note[which, 0]
             for other in range(1, groups):
                 total = total + group_note[which, other]
             sums[which] = total
             block_note[which, col] = total
-
-            def send(s, carry):
-                sum_copy(which, s, col, lax.rem(col + s, blocks)).start()
-                return carry
-
-            lax.fori_loop(1, blocks, send, 0)
+            for step in range(1, blocks):
+                remote(
+                    sums.at[which], block_note.at[which, col],
+                    sum_send.at[which], sum_recv.at[which], (me, lax.rem(col + step, blocks)),
+                ).start()
 
         def read_note(which, count):
-            def step(s, carry):
-                peer = lax.rem(col + blocks - s, blocks)
-                sum_copy(which, s, peer, peer).wait_recv()
-                return carry
-
-            lax.fori_loop(1, blocks, step, 0)
+            wait_bytes(block_note.at[which, pl.ds(0, blocks - 1)], sum_recv.at[which])
             total = block_note[which, 0]
             for other in range(1, blocks):
                 total = total + block_note[which, other]
@@ -371,14 +388,30 @@
         for plane in range(planes):
             z[plane, own, :] = fields[0, plane, own, :]
         mix_own()
-        pl.semaphore_wait(barrier, groups - 1 + 2)
-        mixed_right.start()
-        mixed_left.start()
-        for copy in (fields_right, fields_left, to_right, to_left):
-            copy.start()
+        beside = lax.div(col + blocks - 1, blocks) + lax.div(2 * blocks - 2 - col, blocks)
+        pl.semaphore_wait(barrier, groups - 1 + beside)
+
+        @pl.when(has_right)
+        def _():
+            mixed_right.start()
+            fields_right.start()
+
+        @pl.when(has_left)
+        def _():
+            mixed_left.start()
+            fields_left.start()
+
+        send_halo(0)
         say_hello(0)
-        mixed_right.wait_recv()
-        mixed_left.wait_recv()
+
+        @pl.when(has_left)
+        def _():
+            mixed_right.wait_recv()
+
+        @pl.when(has_right)
+        def _():
+            mixed_left.wait_recv()
+
         hear_hello(0)
         say_hello(1)
 
@@ -394,7 +427,10 @@
         hear_hello(1)
         say_hello(2)
         taps_and_sum(0)
+        hear_hello(2)
+        say_hello(3)
         start_sums(0)
+        send_halo(1, 2)
 
         def square(k, total):
             for half in range(halves):
@@ -404,13 +440,13 @@
 
         norm = all_of(lax.fori_loop(0, members, square, jnp.zeros((width, LANES), F32)))
         mine = finish_sums(0)
-        hear_hello(2)
-        say_hello(3)
-        start_spread(0, True)
+        hear_hello(3)
+        say_hello(4)
+        start_edges(0)
+        start_group(0)
+        send_halo(3)
         send_note(0, [norm, all_of(fields[1, me, own, :] * mine * mine)])
         finish_own(0)
-        hear_hello(3)
-        pass_note(0)
 
         def image_of_first(at):
             for plane in range(planes):
@@ -418,21 +454,33 @@
                     fields[0, plane, at, :] + fields[1, plane, at, :] * full[0, plane, at, :]
                 )
 
-        mixed_right.wait_send()
-        mixed_left.wait_send()
+
+        @pl.when(has_right)
+        def _():
+            mixed_right.wait_send()
+
+        @pl.when(has_left)
+        def _():
+            mixed_left.wait_send()
+
         image_of_first(own)
         mix_own()
-        fields_right.wait_recv()
-        fields_left.wait_recv()
-        has_left = jnp.where(col > 0, 1.0, 0.0)
-        has_right = jnp.where(col < blocks - 1, 1.0, 0.0)
-        for which in range(2):
-            for plane in range(planes):
-                fields[which, plane, low_rows, :] = fields[which, plane, low_rows, :] * has_left
-                fields[which, plane, high_rows, :] = fields[which, plane, high_rows, :] * has_right
+        hear_hello(4)
+        pass_note(0)
         finish_edges(0)
-        to_right.wait_recv()
-        to_left.wait_recv()
+
+        @pl.when(has_left)
+        def _():
+            fields_right.wait_recv()
+            for copy in to_right:
+                copy.wait_recv()
+
+        @pl.when(has_right)
+        def _():
+            fields_left.wait_recv()
+            for copy in to_left:
+                copy.wait_recv()
+
         image_of_first(low_rows)
         image_of_first(high_rows)
         mix_edges()
@@ -440,7 +488,8 @@
         taps_and_sum(1)
         start_sums(1)
         finish_sums(1)
-        start_spread(1, True)
+        start_edges(1)
+        start_group(1)
         norm_0, bend_0 = read_note(0, 2)
         curve_0 = norm_0 + bend_0
         step_0 = norm_0 / curve_0
@@ -479,13 +528,13 @@
             )
         ]
         mine_c = finish_sums(2)
-        start_spread(2, False)
         mine_a = full[0, me, own, :]
         mine_b = mine_a - step_0 * full[1, me, own, :]
         weight = fields[1, me, own, :]
         wb, wc = weight * mine_b, weight * mine_c
         bends = [all_of(v) for v in (wb * mine_a, wc * mine_a, wb * mine_b, wc * mine_b, wc * mine_c)]
         send_note(1, inner + bends)
+        start_group(2)
         pass_note(1)
         g_ab, g_ac, g_bb, g_bc, g_cc, e_ab, e_ac, e_bb, e_bc, e_cc = read_note(1, 10)
         finish_own(2)
@@ -532,40 +581,44 @@
                     in_a * a + in_b * b + in_c * full[2, plane, own, :]
                 )
 
-        for copy in (to_right, to_left, fields_right, fields_left):
-            copy.wait_send()
+        @pl.when(has_right)
+        def _():
+            for copy in to_right:
+                copy.wait_send()
+            fields_right.wait_send()
+
+        @pl.when(has_left)
+        def _():
+            for copy in to_left:
+                copy.wait_send()
+            fields_left.wait_send()
+
         for turn in range(3):
-
-            def settle(s, carry):
-                chunk_copy(turn, s).wait_send()
-                whole_copy(turn, s, me, lax.rem(me + s, groups)).wait_send()
-                return carry
-
-            lax.fori_loop(1, groups, settle, 0)
+            wait_bytes(gathered.at[turn], rs_send.at[turn])
+            wait_bytes(others(turn), ag_send.at[turn])
         for turn in range(2):
 
-            def settle_edges(other, carry):
-                for copy in edge_copies(turn, other, me, me):
-                    copy.wait_send()
-                return carry
-
-            lax.fori_loop(0, groups, settle_edges, 0)
-
-            def settle_notes(s, carry):
-                note_copy(turn, s, me, lax.rem(me + s, groups)).wait_send()
-                return carry
-
-            lax.fori_loop(1, groups, settle_notes, 0)
-
-            def settle_blocks(s, carry):
-                sum_copy(turn, s, col, lax.rem(col + s, blocks)).wait_send()
-                return carry
-
-            lax.fori_loop(1, blocks, settle_blocks, 0)
+            @pl.when(has_right)
+            def _():
+                wait_bytes(full.at[turn, :, low_rows, :], low_send.at[turn])
+
+            @pl.when(has_left)
+            def _():
+                wait_bytes(full.at[turn, :, high_rows, :], high_send.at[turn])
+
+            wait_bytes(group_note.at[turn, pl.ds(0, groups - 1)], note_send.at[turn])
+            wait_bytes(block_note.at[turn, pl.ds(0, blocks - 1)], sum_send.at[turn])
 
     bf16 = jnp.bfloat16
     dma = pltpu.SemaphoreType.DMA
     scratch = [
+        pltpu.SMEM((TAPS,), F32),
+        pltpu.SMEM((2, TAPS), jnp.int32),
+        pltpu.VMEM((obs_rows, LANES), jnp.int32),
+        pltpu.VMEM((obs_rows, LANES), jnp.int32),
+        pltpu.VMEM((obs_rows, LANES), jnp.int32),
+        pltpu.VMEM((obs_rows, LANES), F32),
+        pltpu.VMEM((obs_rows, LANES), F32),
         pltpu.VMEM((levels, members, width, depth), bf16),
         pltpu.VMEM((levels, members, HALO, depth), bf16),
         pltpu.VMEM((levels, members, HALO, depth), bf16),
@@ -581,12 +634,12 @@
         pltpu.VMEM((2, groups, 1, LANES), F32),
         pltpu.VMEM((2, 1, LANES), F32),
         pltpu.VMEM((2, blocks, 1, LANES), F32),
-        pltpu.SemaphoreType.REGULAR((4, 2)),
-        dma,
-        dma((2,)), dma((2,)), dma((2,)), dma((2,)), dma((2,)), dma((2,)),
-        dma((3, groups - 1)), dma((3, groups - 1)), dma((3, groups - 1)), dma((3, groups - 1)),
-        dma((2, groups)), dma((2, groups)), dma((2, groups)), dma((2, groups)),
-        dma((2, groups - 1)), dma((2, groups - 1)), dma((2, blocks - 1)), dma((2, blocks - 1)),
+        pltpu.SemaphoreType.REGULAR((5, 2)),
+        dma((8,)),
+        dma((2,)), dma((2,)), dma((2, levels)), dma((2, levels)), dma((2,)), dma((2,)),
+        dma((3,)), dma((3,)), dma((3,)), dma((3,)),
+        dma((2,)), dma((2,)), dma((2,)), dma((2,)),
+        dma((2,)), dma((2,)), dma((2,)), dma((2,)),
     ]
     return kernel, scratch
 
@@ -599,7 +652,6 @@
         obs_rows = obs_x.shape[0] // LANES
         kernel, scratch = make_kernel(groups, blocks, levels, members, width, depth, obs_rows)
         vmem = pl.BlockSpec(memory_space=pltpu.VMEM)
-        smem = pl.BlockSpec(memory_space=pltpu.SMEM)
         hbm = pl.BlockSpec(memory_space=pl.ANY)
         return pl.pallas_call(
             kernel,
@@ -607,7 +659,7 @@
                 pltpu.VMEM((members, width, depth), F32),
                 pltpu.VMEM((levels, width, depth), F32),
             ),
-            in_specs=[hbm, smem, smem] + [vmem] * 5,
+            in_specs=[hbm] * 8,
             out_specs=(vmem,) * 2,
             scratch_shapes=scratch,
             compiler_params=pltpu.CompilerParams(collective_id=0, has_side_effects=True),

time: 76.7 us -> 71.9 us (0.937)
  Pallas kernels: 74.5 us -> 69.7 us
    pallas_call x1, Pallas kernels: 74.5 us -> 69.7 us  [per_device(): pl.pallas_call(kernel, out_shape=(pltpu.VMEM((members, width, depth), F32...]
where the time goes in v3:
time: 71.9 us; the launch traced here: 71.8 us
  Pallas kernels  69.7 us (97%)
  local copies, waits for them, and re-layouts  1.42 us (2%)
    pallas_call x1, Pallas kernels, per_device(): pl.pallas_call(kernel, out_shape=(pltpu.VMEM((members, width, depth), F32...  69.7 us

profile of v3, /device:TPU:1, one launch (start us, length us, event | category | flops | bytes accessed | tf_op | source)
XLA Modules:
  0.0 71.8 jit_solution(11388530143090033794)
XLA Ops:
  0.6 69.7 %shard_map.95 = (f32[32,16,256]{2,1,0:T(8,128)S(1)}, f32[4,16,256]{2,1,0:T(8,128)S(1)}) custom-call(bf16[4,32,16,256]{3,2,1,0:T(8,128)(2,1)} %pert.1, f32[7]{0:T(128)} %weights_in.1, s32[2,7]{1,0:T(2,128)} %bitcast.11, s32[16,128]{1,0:T(8,128)} %bitcast.6, s32[16,128]{1,0:T(8,128)} %bitcast.7, s32[16,128]{1,0:T(8,128)} %bitcast.8, f32[16,128]{1,0:T(8,128)} %bitcast.9, ...), custom_call_target="tpu_custom_call" | custom-call | tf_op jit(solution)/shard_map/pallas_call | solution.py:656
  70.3 0.8 %copy.12 = f32[32,16,256]{2,1,0:T(8,128)} copy(f32[32,16,256]{2,1,0:T(8,128)S(1)} %get-tuple-element.2) | data formatting | bytes 1048576
  71.1 0.6 copy.13

commit v4 on v3

--- a/solution.py
+++ b/solution.py
@@ -11,7 +11,7 @@
 HALO = 2 * RADIUS
 F32 = jnp.float32
 UNROLL = 4
-TAP_UNROLL = 4
+CHUNK = 8
 MESH = pl.DeviceIdType.MESH
 
 
@@ -19,6 +19,7 @@
     halves = depth // LANES
     planes = levels * halves
     rows = width + 2 * HALO
+    chunks = members // CHUNK
     own = pl.ds(HALO, width)
     low_rows = pl.ds(0, HALO)
     high_rows = pl.ds(HALO + width, HALO)
@@ -29,7 +30,7 @@
         pert, weights_in, offsets_in, obs_x_in, obs_y_in, obs_t_in, innov_in, rinv_in,
         control, increment,
         weights, offsets, obs_x, obs_y, obs_t, innov, rinv,
-        p, p_low, p_high, fields, z, mixed, resid, second, part, gathered, full,
+        p, p_low, p_high, p_right, p_left, mix_out, mix_in, fields, z, mixed, resid, second, part, gathered, full,
         note, group_note, sums, block_note,
         hello, load_sem, mixed_send, mixed_recv, halo_send, halo_recv, field_send, field_recv,
         rs_send, rs_recv, ag_send, ag_recv, low_send, low_recv, high_send, high_recv,
@@ -51,13 +52,14 @@
                 (
                     (obs_x_in, obs_x), (obs_y_in, obs_y), (obs_t_in, obs_t), (innov_in, innov),
                     (rinv_in, rinv), (weights_in, weights), (offsets_in, offsets), (pert, p),
+                    (pert.at[:, :, pl.ds(width - HALO, HALO), :], p_right),
+                    (pert.at[:, :, pl.ds(0, HALO), :], p_left),
                 )
             )
         ]
-        load = loads.pop()
         for copy in loads:
             copy.start()
-        load.start()
+        edge_loads, load, loads = loads[-2:], loads[-3], loads[:-3]
         for step in range(1, groups):
             greet((lax.rem(me + step, groups), col))
 
@@ -92,12 +94,14 @@
         @pl.when(col == 0)
         def _():
             p_low[...] = jnp.zeros(p_low.shape, p_low.dtype)
+            mix_in[0] = jnp.zeros((members, halves, HALO, LANES), F32)
             fields[:, :, low_rows, :] = jnp.zeros((2, planes, HALO, LANES), F32)
             full[:, :, low_rows, :] = jnp.zeros((3, planes, HALO, LANES), F32)
 
         @pl.when(col == blocks - 1)
         def _():
             p_high[...] = jnp.zeros(p_high.shape, p_high.dtype)
+            mix_in[1] = jnp.zeros((members, halves, HALO, LANES), F32)
             fields[:, :, high_rows, :] = jnp.zeros((2, planes, HALO, LANES), F32)
             full[:, :, high_rows, :] = jnp.zeros((3, planes, HALO, LANES), F32)
 
@@ -148,31 +152,43 @@
                 device_id=device, device_id_type=MESH,
             )
 
-        to_right = [
-            remote(
-                pert.at[level, :, pl.ds(width - HALO, HALO), :], p_low.at[level],
-                halo_send.at[0, level], halo_recv.at[0, level], (me, right),
-            )
-            for level in range(levels)
-        ]
-        to_left = [
-            remote(
-                pert.at[level, :, pl.ds(0, HALO), :], p_high.at[level],
-                halo_send.at[1, level], halo_recv.at[1, level], (me, left),
-            )
-            for level in range(levels)
-        ]
+        def members_of(chunk):
+            return pl.ds(chunk * CHUNK, CHUNK)
+
+        def to_right(chunk):
+            return remote(
+                p_right.at[:, members_of(chunk)], p_low.at[:, members_of(chunk)],
+                halo_send.at[0, chunk], halo_recv.at[0, chunk], (me, right),
+            )
+
+        def to_left(chunk):
+            return remote(
+                p_left.at[:, members_of(chunk)], p_high.at[:, members_of(chunk)],
+                halo_send.at[1, chunk], halo_recv.at[1, chunk], (me, left),
+            )
+
+        def mixed_right(chunk):
+            return remote(
+                mix_out.at[0, members_of(chunk)], mix_in.at[0, members_of(chunk)],
+                mixed_send.at[0, chunk], mixed_recv.at[0, chunk], (me, right),
+            )
+
+        def mixed_left(chunk):
+            return remote(
+                mix_out.at[1, members_of(chunk)], mix_in.at[1, members_of(chunk)],
+                mixed_send.at[1, chunk], mixed_recv.at[1, chunk], (me, left),
+            )
 
         def send_halo(*which):
             @pl.when(has_right)
             def _():
-                for level in which:
-                    to_right[level].start()
+                for chunk in which:
+                    to_right(chunk).start()
 
             @pl.when(has_left)
             def _():
-                for level in which:
-                    to_left[level].start()
+                for chunk in which:
+                    to_left(chunk).start()
 
         fields_right = remote(
             fields.at[:, :, last_own, :], fields.at[:, :, low_rows, :],
@@ -182,20 +198,11 @@
             fields.at[:, :, first_own, :], fields.at[:, :, high_rows, :],
             field_send.at[1], field_recv.at[1], (me, left),
         )
-        mixed_right = remote(
-            mixed.at[:, :, last_own, :], mixed.at[:, :, low_rows, :],
-            mixed_send.at[0], mixed_recv.at[0], (me, right),
-        )
-        mixed_left = remote(
-            mixed.at[:, :, first_own, :], mixed.at[:, :, high_rows, :],
-            mixed_send.at[1], mixed_recv.at[1], (me, left),
-        )
-
         tap_weight = [weights[s] for s in range(TAPS)]
         along = [offsets[0, s] for s in range(TAPS)]
         across = [offsets[1, s] for s in range(TAPS)]
 
-        def mix(source, at, k):
+        def mix(source, at, k, out=False):
             for half in range(halves):
                 total = None
                 for level in range(levels):
@@ -204,20 +211,14 @@
                     ]
                     total = term if total is None else total + term
                 mixed[k, half, at, :] = total
-
-        def mix_own():
+                if out:
+                    mix_out[0, k, half] = total[width - HALO :]
+                    mix_out[1, k, half] = total[:HALO]
+
+        def mix_own(out=False):
             def step(k, carry):
                 for more in range(UNROLL):
-                    mix(p, own, UNROLL * k + more)
-                return carry
-
-            lax.fori_loop(0, members // UNROLL, step, 0)
-
-        def mix_edges():
-            def step(k, carry):
-                for more in range(UNROLL):
-                    mix(p_low, low_rows, UNROLL * k + more)
-                    mix(p_high, high_rows, UNROLL * k + more)
+                    mix(p, own, UNROLL * k + more, out)
                 return carry
 
             lax.fori_loop(0, members // UNROLL, step, 0)
@@ -249,41 +250,51 @@
                     total[half] = term if total[half] is None else total[half] + term
             return total
 
-        def transpose_taps(turn):
-            starts = [RADIUS - v for v in along]
-
-            def step(k, carry):
-                for more in range(TAP_UNROLL):
-                    at = TAP_UNROLL * k + more
-                    total = stencil(lambda h, rows_at: mixed[at, h, rows_at, :], starts, reach, back)
+        back_starts = [RADIUS - v for v in along]
+        forth_starts = [HALO + v for v in along]
+
+        def first_edges(chunk):
+            pl.when(has_left)(lambda: mixed_right(chunk).wait_recv())
+            pl.when(has_right)(lambda: mixed_left(chunk).wait_recv())
+            for more in range(CHUNK):
+                k = CHUNK * chunk + more
+                for half in range(halves):
+                    mixed[k, half, low_rows, :] = mix_in[0, k, half]
+                    mixed[k, half, high_rows, :] = mix_in[1, k, half]
+
+        def later_edges(chunk):
+            for more in range(CHUNK):
+                mix(p_low, low_rows, CHUNK * chunk + more)
+                mix(p_high, high_rows, CHUNK * chunk + more)
+
+        def arriving_edges(chunk):
+            pl.when(has_left)(lambda: to_right(chunk).wait_recv())
+            pl.when(has_right)(lambda: to_left(chunk).wait_recv())
+            later_edges(chunk)
+
+        def apply(turn, edges):
+            def step(chunk, so_far):
+                edges(chunk)
+                for more in range(CHUNK):
+                    k = CHUNK * chunk + more
+                    total = stencil(lambda h, rows_at: mixed[k, h, rows_at, :], back_starts, reach, back)
                     for half in range(halves):
-                        resid[turn, at, half, pl.ds(RADIUS, reach), :] = total[half] * keep
-                return carry
-
-            lax.fori_loop(0, members // TAP_UNROLL, step, 0)
-
-        def taps_and_sum(turn):
-            starts = [HALO + v for v in along]
-
-            def step(k, so_far):
-                for more in range(TAP_UNROLL):
-                    at = TAP_UNROLL * k + more
+                        resid[turn, k, half, pl.ds(RADIUS, reach), :] = total[half] * keep
+                for more in range(CHUNK):
+                    k = CHUNK * chunk + more
                     total = stencil(
-                        lambda h, rows_at: resid[turn, at, h, rows_at, :], starts, width, forth
+                        lambda h, rows_at: resid[turn, k, h, rows_at, :], forth_starts, width, forth
                     )
                     so_far = tuple(
                         so_far[level * halves + half]
-                        + p[level, at, :, half * LANES : (half + 1) * LANES].astype(F32) * total[half]
+                        + p[level, k, :, half * LANES : (half + 1) * LANES].astype(F32) * total[half]
                         for level in range(levels)
                         for half in range(halves)
                     )
                 return so_far
 
             summed = lax.fori_loop(
-                0,
-                members // TAP_UNROLL,
-                step,
-                tuple(jnp.zeros((width, LANES), F32) for _ in range(planes)),
+                0, chunks, step, tuple(jnp.zeros((width, LANES), F32) for _ in range(planes))
             )
             for plane in range(planes):
                 part[turn, plane] = summed[plane]
@@ -387,46 +398,33 @@
         load.wait()
         for plane in range(planes):
             z[plane, own, :] = fields[0, plane, own, :]
-        mix_own()
+        mix_own(True)
         beside = lax.div(col + blocks - 1, blocks) + lax.div(2 * blocks - 2 - col, blocks)
         pl.semaphore_wait(barrier, groups - 1 + beside)
 
         @pl.when(has_right)
         def _():
-            mixed_right.start()
+            for chunk in range(chunks):
+                mixed_right(chunk).start()
             fields_right.start()
 
         @pl.when(has_left)
         def _():
-            mixed_left.start()
+            for chunk in range(chunks):
+                mixed_left(chunk).start()
             fields_left.start()
 
+        for copy in edge_loads:
+            copy.wait()
         send_halo(0)
         say_hello(0)
 
-        @pl.when(has_left)
-        def _():
-            mixed_right.wait_recv()
-
-        @pl.when(has_right)
-        def _():
-            mixed_left.wait_recv()
-
         hear_hello(0)
         say_hello(1)
 
-        @pl.when(col == 0)
-        def _():
-            mixed[:, :, low_rows, :] = jnp.zeros((members, halves, HALO, LANES), F32)
-
-        @pl.when(col == blocks - 1)
-        def _():
-            mixed[:, :, high_rows, :] = jnp.zeros((members, halves, HALO, LANES), F32)
-
-        transpose_taps(0)
         hear_hello(1)
         say_hello(2)
-        taps_and_sum(0)
+        apply(0, first_edges)
         hear_hello(2)
         say_hello(3)
         start_sums(0)
@@ -455,14 +453,6 @@
                 )
 
 
-        @pl.when(has_right)
-        def _():
-            mixed_right.wait_send()
-
-        @pl.when(has_left)
-        def _():
-            mixed_left.wait_send()
-
         image_of_first(own)
         mix_own()
         hear_hello(4)
@@ -472,20 +462,14 @@
         @pl.when(has_left)
         def _():
             fields_right.wait_recv()
-            for copy in to_right:
-                copy.wait_recv()
 
         @pl.when(has_right)
         def _():
             fields_left.wait_recv()
-            for copy in to_left:
-                copy.wait_recv()
 
         image_of_first(low_rows)
         image_of_first(high_rows)
-        mix_edges()
-        transpose_taps(1)
-        taps_and_sum(1)
+        apply(1, arriving_edges)
         start_sums(1)
         finish_sums(1)
         start_edges(1)
@@ -506,9 +490,7 @@
         finish_edges(1)
         image_of_second(low_rows)
         image_of_second(high_rows)
-        mix_edges()
-        transpose_taps(2)
-        taps_and_sum(2)
+        apply(2, later_edges)
         start_sums(2)
 
         def products(k, so_far):
@@ -583,15 +565,17 @@
 
         @pl.when(has_right)
         def _():
-            for copy in to_right:
-                copy.wait_send()
             fields_right.wait_send()
+            for chunk in range(chunks):
+                to_right(chunk).wait_send()
+                mixed_right(chunk).wait_send()
 
         @pl.when(has_left)
         def _():
-            for copy in to_left:
-                copy.wait_send()
             fields_left.wait_send()
+            for chunk in range(chunks):
+                to_left(chunk).wait_send()
+                mixed_left(chunk).wait_send()
 
         for turn in range(3):
             wait_bytes(gathered.at[turn], rs_send.at[turn])
@@ -622,6 +606,10 @@
         pltpu.VMEM((levels, members, width, depth), bf16),
         pltpu.VMEM((levels, members, HALO, depth), bf16),
         pltpu.VMEM((levels, members, HALO, depth), bf16),
+        pltpu.VMEM((levels, members, HALO, depth), bf16),
+        pltpu.VMEM((levels, members, HALO, depth), bf16),
+        pltpu.VMEM((2, members, halves, HALO, LANES), F32),
+        pltpu.VMEM((2, members, halves, HALO, LANES), F32),
         pltpu.VMEM((2, planes, rows, LANES), F32),
         pltpu.VMEM((planes, rows, LANES), F32),
         pltpu.VMEM((members, halves, rows, LANES), F32),
@@ -635,8 +623,8 @@
         pltpu.VMEM((2, 1, LANES), F32),
         pltpu.VMEM((2, blocks, 1, LANES), F32),
         pltpu.SemaphoreType.REGULAR((5, 2)),
-        dma((8,)),
-        dma((2,)), dma((2,)), dma((2, levels)), dma((2, levels)), dma((2,)), dma((2,)),
+        dma((10,)),
+        dma((2, chunks)), dma((2, chunks)), dma((2, chunks)), dma((2, chunks)), dma((2,)), dma((2,)),
         dma((3,)), dma((3,)), dma((3,)), dma((3,)),
         dma((2,)), dma((2,)), dma((2,)), dma((2,)),
         dma((2,)), dma((2,)), dma((2,)), dma((2,)),

time: 71.9 us -> 68.3 us (0.950)
  Pallas kernels: 69.7 us -> 66.1 us
    pallas_call x1, Pallas kernels: 69.7 us -> 66.1 us  [per_device(): pl.pallas_call(kernel, out_shape=(pltpu.VMEM((members, width, depth), F32...]
where the time goes in v4:
time: 68.3 us; the launch traced here: 68.2 us
  Pallas kernels  66.1 us (97%)
  local copies, waits for them, and re-layouts  1.42 us (2%)
    pallas_call x1, Pallas kernels, per_device(): pl.pallas_call(kernel, out_shape=(pltpu.VMEM((members, width, depth), F32...  66.1 us
    unnamed x2, local copies, waits for them, and re-layouts  1.42 us

profile of v4, /device:TPU:1, one launch (start us, length us, event | category | flops | bytes accessed | tf_op | source)
XLA Modules:
  0.0 68.2 jit_solution(4605772270230782749)
XLA Ops:
  0.6 66.1 %shard_map.95 = (f32[32,16,256]{2,1,0:T(8,128)S(1)}, f32[4,16,256]{2,1,0:T(8,128)S(1)}) custom-call(bf16[4,32,16,256]{3,2,1,0:T(8,128)(2,1)} %pert.1, f32[7]{0:T(128)} %weights_in.1, s32[2,7]{1,0:T(2,128)} %bitcast.11, s32[16,128]{1,0:T(8,128)} %bitcast.6, s32[16,128]{1,0:T(8,128)} %bitcast.7, s32[16,128]{1,0:T(8,128)} %bitcast.8, f32[16,128]{1,0:T(8,128)} %bitcast.9, ...), custom_call_target="tpu_custom_call" | custom-call | tf_op jit(solution)/shard_map/pallas_call | solution.py:644
  66.7 0.8 %copy.12 = f32[32,16,256]{2,1,0:T(8,128)} copy(f32[32,16,256]{2,1,0:T(8,128)S(1)} %get-tuple-element.2) | data formatting | bytes 1048576
  67.5 0.6 copy.13

commit v5 on v4

--- a/solution.py
+++ b/solution.py
@@ -11,6 +11,7 @@
 HALO = 2 * RADIUS
 F32 = jnp.float32
 UNROLL = 4
+OBS_UNROLL = 4
 CHUNK = 8
 MESH = pl.DeviceIdType.MESH
 
@@ -46,6 +47,17 @@
         def greet(target):
             pl.semaphore_signal(barrier, inc=1, device_id=target, device_id_type=MESH)
 
+        for step in range(1, groups):
+            greet((lax.rem(me + step, groups), col))
+
+        @pl.when(has_right)
+        def _():
+            greet((me, right))
+
+        @pl.when(has_left)
+        def _():
+            greet((me, left))
+
         loads = [
             pltpu.make_async_copy(source, target, load_sem.at[at])
             for at, (source, target) in enumerate(
@@ -60,17 +72,6 @@
         for copy in loads:
             copy.start()
         edge_loads, load, loads = loads[-2:], loads[-3], loads[:-3]
-        for step in range(1, groups):
-            greet((lax.rem(me + step, groups), col))
-
-        @pl.when(has_right)
-        def _():
-            greet((me, right))
-
-        @pl.when(has_left)
-        def _():
-            greet((me, left))
-
         def hello_sides(turn):
             away = 1 << turn
             return (0, col + away, col + away < blocks), (1, col - away, col >= away)
@@ -91,46 +92,39 @@
                 def _():
                     pl.semaphore_wait(hello.at[turn, 1 - side], 1)
 
-        @pl.when(col == 0)
-        def _():
-            p_low[...] = jnp.zeros(p_low.shape, p_low.dtype)
-            mix_in[0] = jnp.zeros((members, halves, HALO, LANES), F32)
-            fields[:, :, low_rows, :] = jnp.zeros((2, planes, HALO, LANES), F32)
-            full[:, :, low_rows, :] = jnp.zeros((3, planes, HALO, LANES), F32)
-
-        @pl.when(col == blocks - 1)
-        def _():
-            p_high[...] = jnp.zeros(p_high.shape, p_high.dtype)
-            mix_in[1] = jnp.zeros((members, halves, HALO, LANES), F32)
-            fields[:, :, high_rows, :] = jnp.zeros((2, planes, HALO, LANES), F32)
-            full[:, :, high_rows, :] = jnp.zeros((3, planes, HALO, LANES), F32)
-
         lanes8 = lax.broadcasted_iota(jnp.int32, (1, LANES), 1)
         cell_rows = lax.broadcasted_iota(jnp.int32, (levels * width, LANES), 0)
         depth_rows = lax.broadcasted_iota(jnp.int32, (depth, LANES), 0)
 
         def place(chunk, total):
-            at = pl.ds(chunk, 1)
-            cell = obs_t[at, :] * width + (obs_x[at, :] - col * width)
-            r = rinv[at, :]
-            hit = cell_rows == cell
-            pieces = []
-            for value in (r * innov[at, :], r):
-                rest = value
-                for _ in range(3):
-                    piece = rest.astype(jnp.bfloat16)
-                    rest = rest - piece.astype(F32)
-                    pieces.append(jnp.where(hit, piece.astype(F32), 0.0).astype(jnp.bfloat16))
-            left_side = jnp.concatenate(pieces, axis=0)
-            right_side = jnp.where(depth_rows == obs_y[at, :], 1.0, 0.0).astype(jnp.bfloat16)
+            left_side, right_side = [], []
+            for more in range(OBS_UNROLL):
+                at = pl.ds(chunk * OBS_UNROLL + more, 1)
+                cell = obs_t[at, :] * width + (obs_x[at, :] - col * width)
+                r = rinv[at, :]
+                hit = cell_rows == cell
+                pieces = []
+                for value in (r * innov[at, :], r):
+                    rest = value
+                    for _ in range(3):
+                        piece = rest.astype(jnp.bfloat16)
+                        rest = rest - piece.astype(F32)
+                        pieces.append(jnp.where(hit, piece.astype(F32), 0.0).astype(jnp.bfloat16))
+                left_side.append(jnp.concatenate(pieces, axis=0))
+                right_side.append(
+                    jnp.where(depth_rows == obs_y[at, :], 1.0, 0.0).astype(jnp.bfloat16)
+                )
             return total + lax.dot_general(
-                left_side, right_side, (((1,), (1,)), ((), ())), preferred_element_type=F32
+                jnp.concatenate(left_side, axis=1),
+                jnp.concatenate(right_side, axis=1),
+                (((1,), (1,)), ((), ())),
+                preferred_element_type=F32,
             )
 
         for copy in loads:
             copy.wait()
         spread = lax.fori_loop(
-            0, obs_rows, place, jnp.zeros((6 * levels * width, depth), F32)
+            0, obs_rows // OBS_UNROLL, place, jnp.zeros((6 * levels * width, depth), F32)
         )
         cells = levels * width
         for which in range(2):
@@ -418,6 +412,20 @@
             copy.wait()
         send_halo(0)
         say_hello(0)
+
+        @pl.when(col == 0)
+        def _():
+            p_low[...] = jnp.zeros(p_low.shape, p_low.dtype)
+            mix_in[0] = jnp.zeros((members, halves, HALO, LANES), F32)
+            fields[:, :, low_rows, :] = jnp.zeros((2, planes, HALO, LANES), F32)
+            full[:, :, low_rows, :] = jnp.zeros((3, planes, HALO, LANES), F32)
+
+        @pl.when(col == blocks - 1)
+        def _():
+            p_high[...] = jnp.zeros(p_high.shape, p_high.dtype)
+            mix_in[1] = jnp.zeros((members, halves, HALO, LANES), F32)
+            fields[:, :, high_rows, :] = jnp.zeros((2, planes, HALO, LANES), F32)
+            full[:, :, high_rows, :] = jnp.zeros((3, planes, HALO, LANES), F32)
 
         hear_hello(0)
         say_hello(1)
@@ -641,7 +649,7 @@
         kernel, scratch = make_kernel(groups, blocks, levels, members, width, depth, obs_rows)
         vmem = pl.BlockSpec(memory_space=pltpu.VMEM)
         hbm = pl.BlockSpec(memory_space=pl.ANY)
-        return pl.pallas_call(
+        kept = pl.pallas_call(
             kernel,
             out_shape=(
                 pltpu.VMEM((members, width, depth), F32),
@@ -656,6 +664,27 @@
             *(v.reshape(obs_rows, LANES) for v in (obs_x, obs_y, obs_t, innovations, obs_rinv)),
         )
 
+        def put_out(control, increment, control_out, increment_out, sem):
+            copies = [
+                pltpu.make_async_copy(control, control_out, sem.at[0]),
+                pltpu.make_async_copy(increment, increment_out, sem.at[1]),
+            ]
+            for copy in copies:
+                copy.start()
+            for copy in copies:
+                copy.wait()
+
+        return pl.pallas_call(
+            put_out,
+            out_shape=(
+                jax.ShapeDtypeStruct((members, width, depth), F32),
+                jax.ShapeDtypeStruct((levels, width, depth), F32),
+            ),
+            in_specs=[vmem] * 2,
+            out_specs=(pl.BlockSpec(memory_space=pltpu.HBM),) * 2,
+            scratch_shapes=[pltpu.SemaphoreType.DMA((2,))],
+        )(*(pltpu.with_memory_space_constraint(v, pltpu.VMEM) for v in kept))
+
     return jax.shard_map(
         per_device,
         mesh=mesh,

time: 68.3 us -> 65.8 us (0.963)
  local copies, waits for them, and re-layouts: 1.42 us -> 0 us
  Pallas kernels: 66.1 us -> 65.1 us
    pallas_call x1, Pallas kernels: 66.1 us -> 64.2 us  [per_device(): pl.pallas_call(kernel, out_shape=(pltpu.VMEM((members, width, depth), F32...]
    unnamed x2 -> x0, local copies, waits for them, and re-layouts: 1.42 us -> none
    pallas_call x0 -> x1, Pallas kernels: none -> 0.82 us  [per_device(): pl.pallas_call(put_out, out_shape=(jax.ShapeDtypeStruct((members, width,...]
where the time goes in v5:
time: 65.8 us; the launch traced here: 65.7 us
  Pallas kernels  65.1 us (99%)
    pallas_call x1, Pallas kernels, per_device(): pl.pallas_call(kernel, out_shape=(pltpu.VMEM((members, width, depth), F32...  64.2 us

profile of v5, /device:TPU:1, one launch (start us, length us, event | category | flops | bytes accessed | tf_op | source)
XLA Modules:
  0.0 65.7 jit_solution(17644967550502715606)
XLA Ops:
  0.6 64.2 %shard_map.95 = (f32[32,16,256]{2,1,0:T(8,128)S(1)}, f32[4,16,256]{2,1,0:T(8,128)S(1)}) custom-call(bf16[4,32,16,256]{3,2,1,0:T(8,128)(2,1)} %pert.1, f32[7]{0:T(128)} %weights_in.1, s32[2,7]{1,0:T(2,128)} %bitcast.11, s32[16,128]{1,0:T(8,128)} %bitcast.6, s32[16,128]{1,0:T(8,128)} %bitcast.7, s32[16,128]{1,0:T(8,128)} %bitcast.8, f32[16,128]{1,0:T(8,128)} %bitcast.9, ...), custom_call_target="tpu_custom_call" | custom-call | tf_op jit(solution)/shard_map/pallas_call | solution.py:652
  64.9 0.8 %shard_map.96 = (f32[32,16,256]{2,1,0:T(8,128)}, f32[4,16,256]{2,1,0:T(8,128)}) custom-call(f32[32,16,256]{2,1,0:T(8,128)S(1)} %get-tuple-element.4.control, f32[4,16,256]{2,1,0:T(8,128)S(1)} %get-tuple-element.5.increment), custom_call_target="tpu_custom_call" | custom-call | tf_op jit(solution)/shard_map/pallas_call | solution.py:677

commit v6 on v5

--- a/solution.py
+++ b/solution.py
@@ -436,7 +436,7 @@
         hear_hello(2)
         say_hello(3)
         start_sums(0)
-        send_halo(1, 2)
+        send_halo(1)
 
         def square(k, total):
             for half in range(halves):
@@ -450,7 +450,7 @@
         say_hello(4)
         start_edges(0)
         start_group(0)
-        send_halo(3)
+        send_halo(2, 3)
         send_note(0, [norm, all_of(fields[1, me, own, :] * mine * mine)])
         finish_own(0)
 

time: 65.8 us -> 65.5 us (level)
  no operation moved by 1% of the time
where the time goes in v6:
time: 65.5 us; the launch traced here: 65.3 us
  Pallas kernels  64.7 us (99%)
    pallas_call x1, Pallas kernels, per_device(): pl.pallas_call(kernel, out_shape=(pltpu.VMEM((members, width, depth), F32...  63.9 us

profile of v6, /device:TPU:1, one launch (start us, length us, event | category | flops | bytes accessed | tf_op | source)
XLA Modules:
  0.0 65.3 jit_solution(10208406880563427658)
XLA Ops:
  0.6 63.9 %shard_map.95 = (f32[32,16,256]{2,1,0:T(8,128)S(1)}, f32[4,16,256]{2,1,0:T(8,128)S(1)}) custom-call(bf16[4,32,16,256]{3,2,1,0:T(8,128)(2,1)} %pert.1, f32[7]{0:T(128)} %weights_in.1, s32[2,7]{1,0:T(2,128)} %bitcast.11, s32[16,128]{1,0:T(8,128)} %bitcast.6, s32[16,128]{1,0:T(8,128)} %bitcast.7, s32[16,128]{1,0:T(8,128)} %bitcast.8, f32[16,128]{1,0:T(8,128)} %bitcast.9, ...), custom_call_target="tpu_custom_call" | custom-call | tf_op jit(solution)/shard_map/pallas_call | solution.py:652
  64.5 0.8 %shard_map.96 = (f32[32,16,256]{2,1,0:T(8,128)}, f32[4,16,256]{2,1,0:T(8,128)}) custom-call(f32[32,16,256]{2,1,0:T(8,128)S(1)} %get-tuple-element.4.control, f32[4,16,256]{2,1,0:T(8,128)S(1)} %get-tuple-element.5.increment), custom_call_target="tpu_custom_call" | custom-call | tf_op jit(solution)/shard_map/pallas_call | solution.py:677
